TPU v7x, 128 devices: a whole 4x4x4 slice. The times are simulated.
128 devices in a mesh: ice: 8 (over x, core), ocn: 16 (over z, y).
Axes of the slice: x: 4, y: 4, z: 4, core: 2. Of those that a mesh axis runs over, the one named last changes fastest.
Arguments:
- ice_state: bfloat16 [5, 20, 131072], P(None, None, ('ice', 'ocn')), may hold values from -6 to 6
- ocean_state: bfloat16 [5, 20, 131072], P(None, None, ('ice', 'ocn')), may hold values from -5 to 5
- ice_rate: float32 [5, 20], replicated, may hold values from 0.2 to 2
- block_weights: bfloat16 [16384, 128, 128], P(('ice', 'ocn')), may hold values from -0.1875 to 0.1875
- block_route: int32 [16384, 1], P(('ice', 'ocn')), may hold values from 0 to 127; in each aligned block of 128 rows (0 to 127, 128 to 255, ...) at most 2 rows name the same one
- block_tiles: int32 [16384, 2], P(('ice', 'ocn')), may hold values from 0 to 7
- block_valid: int32 [16384], P(('ice', 'ocn')), may hold values from 16 to 128
- ice_mask: int32 [131072], P(('ice', 'ocn')), may hold values 0 or 1
Outputs:
- ice_final: bfloat16 [5, 20, 131072], P(None, None, ('ice', 'ocn'))
- ocean_flux: bfloat16 [5, 20, 131072], P(None, None, ('ice', 'ocn'))
Inputs may be any that keep to these rules, and one draw needn't show every extreme that they name: `block_route`: among the blocks of one device no destination appears more than 2 times.
All inputs are finite; a program needn't handle non-finite values. No bound on the sum of `ice_mask` on one device may be relied on, other than what follows from the above.
Results may differ from a plain program's by a relative error of at most 0.008.
Values may be sent and summed in bfloat16 or wider, within the bound.
A program may use at most 128 MiB of HBM per device.

v0:
```python
import jax
import jax.numpy as jnp
from jax import lax
from jax.sharding import PartitionSpec as P

CAP = 2


def forward_move(buffer):
    return lax.all_to_all(buffer, ("ice", "ocn"), split_axis=0, concat_axis=0, tiled=True)


def back_move(buffer):
    return lax.all_to_all(buffer, ("ice", "ocn"), split_axis=0, concat_axis=0, tiled=True)


def on_device(
    ice_state, ocean_state, ice_rate, block_weights, block_route, block_tiles, block_valid, ice_mask
):
    cats, fields, cells = ice_state.shape
    chans = cats * fields
    blocks, width, unused = block_weights.shape
    tiles = cells // width
    devices = lax.axis_size(("ice", "ocn"))
    route = block_route[:, 0]
    source = block_tiles[:, 0]
    target = block_tiles[:, 1]
    order = jnp.arange(blocks, dtype=jnp.int32)
    earlier = (route[None, :] == route[:, None]) & (order[None, :] < order[:, None])
    slot = jnp.sum(earlier.astype(jnp.int32), axis=1)
    place = route * CAP + slot
    live = jnp.arange(width, dtype=jnp.int32)[None, :] < block_valid[:, None]
    masked = jnp.where(live[:, :, None], block_weights, jnp.zeros((), jnp.bfloat16))
    meta_send = (
        jnp.full((devices * CAP,), -1, jnp.int32).at[place].set(target).reshape(devices, CAP)
    )
    meta = lax.all_to_all(
        meta_send, ("ice", "ocn"), split_axis=0, concat_axis=0, tiled=True
    ).reshape(devices * CAP)
    tile_ids = jnp.arange(tiles, dtype=jnp.int32)
    picker_ocean = (meta[None, :] == tile_ids[:, None]).astype(jnp.bfloat16)
    picker_ice = (source[None, :] == tile_ids[:, None]).astype(jnp.float32)
    rates = ice_rate.reshape(chans, 1)
    land = ice_mask.astype(jnp.float32)[None, :]
    ocean = ocean_state.reshape(chans, cells).astype(jnp.float32)
    ice = (ice_state * ice_mask.astype(jnp.bfloat16)[None, None, :]).reshape(chans, cells)
    flux = ocean_state.reshape(chans, cells)
    for turn in range(2):
        picked = ice.reshape(chans, tiles, width)[:, source, :]
        prods = jnp.einsum(
            "cbi,bio->bco", picked, masked, preferred_element_type=jnp.float32
        ).astype(jnp.bfloat16)
        outgoing = jnp.zeros((devices * CAP, chans, width), jnp.bfloat16).at[place].set(prods)
        arrived = forward_move(outgoing.reshape(devices, CAP, chans, width)).reshape(
            devices * CAP, chans, width
        )
        ocean_in = jnp.einsum(
            "tk,kcj->ctj", picker_ocean, arrived, preferred_element_type=jnp.float32
        ).reshape(chans, cells)
        flux = jnp.tanh(ocean_in + ocean).astype(jnp.bfloat16)
        flux_tiles = flux.reshape(chans, tiles, width)
        replies = jnp.einsum(
            "tk,ctj->kcj", picker_ocean, flux_tiles, preferred_element_type=jnp.float32
        ).astype(jnp.bfloat16)
        returned = back_move(replies.reshape(devices, CAP, chans, width)).reshape(
            devices * CAP, chans, width
        )
        taken = returned[place]
        contrib = jnp.einsum("bco,bio->bci", taken, masked, preferred_element_type=jnp.float32)
        forcing = jnp.einsum("tb,bci->cti", picker_ice, contrib).reshape(chans, cells)
        ice = (land * (ice.astype(jnp.float32) + rates * jnp.tanh(forcing))).astype(jnp.bfloat16)
    return (ice.reshape(cats, fields, cells), flux.reshape(cats, fields, cells))


def solution(mesh):
    placed = (
        P(None, None, ("ice", "ocn")),
        P(None, None, ("ice", "ocn")),
        P(),
        P(("ice", "ocn"), None, None),
        P(("ice", "ocn"), None),
        P(("ice", "ocn"), None),
        P(("ice", "ocn")),
        P(("ice", "ocn")),
    )
    return jax.shard_map(
        on_device,
        mesh=mesh,
        in_specs=placed,
        out_specs=(P(None, None, ("ice", "ocn")), P(None, None, ("ice", "ocn"))),
        check_vma=False,
    )
```

profile of v0, /device:TPU:0, one launch (start us, length us, event | category | flops | bytes accessed | tf_op | source)
XLA Modules:
  0.0 527.8 jit_solution(163115170659308400)
XLA Ops:
  0.6 0.9 convert_reduce_fusion
  1.5 0.8 slice_bitcast_fusion.1
  2.3 1.0 scatter_custom_fusion
  3.3 0.8 all_to_all.18
  4.1 11.2 %all-to-all-start = ((s32[128,1,2]{2,1,0:T(1,128)}), s32[128,1,2]{2,1,0:T(1,128)S(1)}, u32[]{:S(2)}, u32[]{:S(2)}) async-start(s32[128,1,2]{2,1,0:T(1,128)} %bitcast.4), calls=%async_computation | async-start | bytes 131072 | tf_op jit(solution)/shard_map/all_to_all | solution.py:37
  15.2 0.8 fusion.57
  16.0 1.0 broadcast_multiply_fusion
  17.0 0.1 reshape_reshape.3
  17.2 0.8 iota_compare_fusion
  18.0 2.8 gather_fusion
  20.7 5.7 %fusion.10 = bf16[128,100,128]{2,1,0:T(8,128)(2,1)S(1)} fusion(bf16[128,128,128]{2,1,0:T(8,128)(2,1)} %param.11, pred[128,128]{1,0:T(8,128)(4,1)S(1)} %iota_compare_fusion, bf16[128,100,128]{2,1,0:T(8,128)(2,1)} %gather_fusion), kind=kOutput, calls=%fused_computation.20 | convolution fusion | flops 423165952 | bytes 10764288 | tf_op jit(solution)/shard_map/cbi,bio->bco/dot_general | solution.py:50
  26.4 3.7 broadcast.57.clone
  30.1 16.4 %scatter_fusion = bf16[256,100,128]{2,1,0:T(8,128)(2,1)} fusion(bf16[256,100,128]{2,1,0:T(8,128)(2,1)} %broadcast.57.clone, s32[128]{0:T(128)S(1)} %get-tuple-element.10, bf16[128,100,128]{2,1,0:T(8,128)(2,1)S(1)} %fusion.10), kind=kCustom, calls=%fused_computation.5 | custom fusion | bytes 9830912 | tf_op jit(solution)/shard_map/scatter | solution.py:53
  46.5 10.9 %copy.32 = bf16[128,2,100,128]{3,1,2,0:T(2,128)(2,1)} copy(bf16[128,2,100,128]{3,2,1,0:T(8,128)(2,1)} %bitcast.72) | data formatting | bytes 13107200 | tf_op jit(solution)/shard_map/reshape | solution.py:54
  57.4 10.2 %all-to-all-start.1 = ((bf16[128,2,100,128]{3,1,2,0:T(2,128)(2,1)}), bf16[128,2,100,128]{3,1,2,0:T(2,128)(2,1)}, u32[]{:S(2)}, u32[]{:S(2)}) async-start(bf16[128,2,100,128]{3,1,2,0:T(2,128)(2,1)} %copy.32), calls=%async_computation.1 | async-start | bytes 13107200 | tf_op jit(solution)/shard_map/all_to_all | solution.py:10
  67.8 0.5 broadcast.78
  68.3 0.8 reduce.3
  69.1 0.1 eq.49
  69.2 82.1 %all-to-all-done.1 = bf16[128,2,100,128]{3,1,2,0:T(2,128)(2,1)} async-done(((bf16[128,2,100,128]{3,1,2,0:T(2,128)(2,1)}), bf16[128,2,100,128]{3,1,2,0:T(2,128)(2,1)}, u32[]{:S(2)}, u32[]{:S(2)}) %all-to-all-start.1) | async-done | bytes 6553632 | tf_op jit(solution)/shard_map/all_to_all | solution.py:10
  151.3 6.9 %copy.33 = bf16[128,2,100,128]{3,1,0,2:T(2,128)(2,1)} copy(bf16[128,2,100,128]{3,1,2,0:T(2,128)(2,1)} %all-to-all-done.1) | data formatting | bytes 13107200 | tf_op jit(solution)/shard_map/all_to_all | solution.py:10
  158.2 8.2 %convolution_convert_fusion.1 = bf16[256,100,128]{2,0,1:T(8,128)(2,1)} fusion(f32[100,8,128]{2,1,0:T(8,128)S(1)} %reshape.122, bf16[256,100,128]{2,0,1:T(8,128)(2,1)} %bitcast.74, s32[256]{0:T(256)S(1)} %eq.49), kind=kOutput, calls=%fused_computation.8 | convolution fusion | flops 108343296 | bytes 13517824 | tf_op jit(solution)/shard_map/tk,ctj->kcj/dot_general | solution.py:62
  166.4 6.8 %copy.34 = bf16[128,2,100,128]{3,1,2,0:T(2,128)(2,1)} copy(bf16[128,2,100,128]{3,1,0,2:T(2,128)(2,1)} %bitcast.75) | data formatting | bytes 13107200 | tf_op jit(solution)/shard_map/reshape | solution.py:65
  173.2 6.2 %all-to-all-start.2 = ((bf16[128,2,100,128]{3,1,2,0:T(2,128)(2,1)}), bf16[128,2,100,128]{3,1,2,0:T(2,128)(2,1)}, u32[]{:S(2)}, u32[]{:S(2)}) async-start(bf16[128,2,100,128]{3,1,2,0:T(2,128)(2,1)} %copy.34), calls=%async_computation.2 | async-start | bytes 13107200 | tf_op jit(solution)/shard_map/all_to_all | solution.py:14
  179.5 83.1 %all-to-all-done.2 = bf16[128,2,100,128]{3,1,2,0:T(2,128)(2,1)} async-done(((bf16[128,2,100,128]{3,1,2,0:T(2,128)(2,1)}), bf16[128,2,100,128]{3,1,2,0:T(2,128)(2,1)}, u32[]{:S(2)}, u32[]{:S(2)}) %all-to-all-start.2) | async-done | bytes 6553632 | tf_op jit(solution)/shard_map/all_to_all | solution.py:14
  262.6 6.8 %copy.35 = bf16[128,2,100,128]{3,2,1,0:T(8,128)(2,1)} copy(bf16[128,2,100,128]{3,1,2,0:T(2,128)(2,1)} %all-to-all-done.2) | data formatting | bytes 13107200 | tf_op jit(solution)/shard_map/all_to_all | solution.py:14
  269.4 5.7 %gather_fusion.1 = bf16[128,100,128]{2,1,0:T(8,128)(2,1)} fusion(bf16[256,100,128]{2,1,0:T(8,128)(2,1)} %bitcast.78, s32[1024]{0:T(1024)S(1)} %pad_clamp_fusion), kind=kCustom, calls=%fused_computation.1 | custom fusion | bytes 6554112 | tf_op jit(solution)/shard_map/gather | solution.py:68
  275.2 5.7 %fusion.9 = bf16[128,100,128]{2,1,0:T(8,128)(2,1)S(1)} fusion(bf16[128,100,128]{2,1,0:T(8,128)(2,1)} %gather_fusion.1, bf16[128,128,128]{2,1,0:T(8,128)(2,1)} %param.11, pred[128,128]{1,0:T(8,128)(4,1)S(1)} %iota_compare_fusion), kind=kOutput, calls=%fused_computation.19 | convolution fusion | flops 421527552 | bytes 10764288 | tf_op jit(solution)/shard_map/bco,bio->bci/dot_general | solution.py:69
  280.8 0.5 fusion.33
  281.4 2.8 gather_fusion.2
  284.2 6.9 %fusion.13 = bf16[128,100,128]{2,1,0:T(8,128)(2,1)} fusion(bf16[128,128,128]{2,1,0:T(8,128)(2,1)} %param.11, pred[128,128]{1,0:T(8,128)(4,1)S(1)} %iota_compare_fusion, bf16[128,100,128]{2,1,0:T(8,128)(2,1)} %gather_fusion.2), kind=kOutput, calls=%fused_computation.21 | convolution fusion | flops 423165952 | bytes 10764288 | tf_op jit(solution)/shard_map/cbi,bio->bco/dot_general | solution.py:50
  291.1 3.7 broadcast.57
  294.7 18.9 %scatter_fusion.1 = bf16[256,100,128]{2,1,0:T(8,128)(2,1)} fusion(bf16[256,100,128]{2,1,0:T(8,128)(2,1)} %broadcast.57, s32[128]{0:T(128)S(1)} %get-tuple-element.10, bf16[128,100,128]{2,1,0:T(8,128)(2,1)} %fusion.13), kind=kCustom, calls=%fused_computation.6 | custom fusion | bytes 9830912 | tf_op jit(solution)/shard_map/scatter | solution.py:53
  313.6 10.1 %copy.38 = bf16[128,2,100,128]{3,1,2,0:T(2,128)(2,1)S(1)} copy(bf16[128,2,100,128]{3,2,1,0:T(8,128)(2,1)} %bitcast.71) | data formatting | bytes 13107200 | tf_op jit(solution)/shard_map/reshape | solution.py:54
  323.7 82.4 %all_to_all.29 = bf16[128,2,100,128]{3,1,2,0:T(2,128)(2,1)S(1)} all-to-all(bf16[128,2,100,128]{3,1,2,0:T(2,128)(2,1)S(1)} %copy.38), channel_id=1, replica_groups=mesh['ice'=8,'ocn'=16] {'ice','ocn'}, dimensions={0} | all-to-all | bytes 13107200 | tf_op jit(solution)/shard_map/all_to_all | solution.py:10
  406.1 5.8 %copy.39 = bf16[128,2,100,128]{3,1,0,2:T(2,128)(2,1)S(1)} copy(bf16[128,2,100,128]{3,1,2,0:T(2,128)(2,1)S(1)} %all_to_all.29) | data formatting | bytes 13107200 | tf_op jit(solution)/shard_map/all_to_all | solution.py:10
  411.9 1.0 convolution_bitcast_fusion
  412.8 1.9 convolution_convert_fusion
  414.8 5.8 %copy.40 = bf16[128,2,100,128]{3,1,2,0:T(2,128)(2,1)} copy(bf16[128,2,100,128]{3,1,0,2:T(2,128)(2,1)S(1)} %bitcast.73) | data formatting | bytes 13107200 | tf_op jit(solution)/shard_map/reshape | solution.py:65
  420.5 6.1 %all-to-all-start.4 = ((bf16[128,2,100,128]{3,1,2,0:T(2,128)(2,1)}), bf16[128,2,100,128]{3,1,2,0:T(2,128)(2,1)}, u32[]{:S(2)}, u32[]{:S(2)}) async-start(bf16[128,2,100,128]{3,1,2,0:T(2,128)(2,1)} %copy.40), calls=%async_computation.4 | async-start | bytes 13107200 | tf_op jit(solution)/shard_map/all_to_all | solution.py:14
  426.6 0.8 tanh.36
  427.5 0.8 tanh_convert_fusion
  428.3 81.5 %all-to-all-done.4 = bf16[128,2,100,128]{3,1,2,0:T(2,128)(2,1)} async-done(((bf16[128,2,100,128]{3,1,2,0:T(2,128)(2,1)}), bf16[128,2,100,128]{3,1,2,0:T(2,128)(2,1)}, u32[]{:S(2)}, u32[]{:S(2)}) %all-to-all-start.4) | async-done | bytes 6553632 | tf_op jit(solution)/shard_map/all_to_all | solution.py:14
  509.8 6.8 %copy.41 = bf16[128,2,100,128]{3,2,1,0:T(8,128)(2,1)} copy(bf16[128,2,100,128]{3,1,2,0:T(2,128)(2,1)} %all-to-all-done.4) | data formatting | bytes 13107200 | tf_op jit(solution)/shard_map/all_to_all | solution.py:14
  516.6 4.2 gather_fusion.3
  520.7 5.1 fusion.8
  525.8 0.5 fusion.26
  526.4 0.4 copy-done
  526.9 0.9 multiply_convert_fusion
  (20 shorter events, 0.5 us)
Async XLA Ops:
  4.1 53.3 %all-to-all-start = ((s32[128,1,2]{2,1,0:T(1,128)}), s32[128,1,2]{2,1,0:T(1,128)S(1)}, u32[]{:S(2)}, u32[]{:S(2)}) async-start(s32[128,1,2]{2,1,0:T(1,128)} %bitcast.4), calls=%async_computation | async-start | bytes 131072 | tf_op jit(solution)/shard_map/all_to_all | solution.py:37
  17.1 0.8 copy-start.3
  57.4 10.3 %copy-start.2 = (bf16[5,20,1024]{2,1,0:T(8,128)(2,1)S(1)}, bf16[5,20,1024]{2,1,0:T(8,128)(2,1)}, u32[]{:S(2)}) copy-start(bf16[5,20,1024]{2,1,0:T(8,128)(2,1)} %param.9) | copy-start | bytes 614404
  57.4 94.0 %all-to-all-start.1 = ((bf16[128,2,100,128]{3,1,2,0:T(2,128)(2,1)}), bf16[128,2,100,128]{3,1,2,0:T(2,128)(2,1)}, u32[]{:S(2)}, u32[]{:S(2)}) async-start(bf16[128,2,100,128]{3,1,2,0:T(2,128)(2,1)} %copy.32), calls=%async_computation.1 | async-start | bytes 13107200 | tf_op jit(solution)/shard_map/all_to_all | solution.py:10
  173.2 6.2 %copy-start.5 = (f32[5,20]{1,0:T(8,128)S(1)}, f32[5,20]{1,0:T(8,128)}, u32[]{:S(2)}) copy-start(f32[5,20]{1,0:T(8,128)} %param.10) | copy-start | bytes 1204
  173.2 89.4 %all-to-all-start.2 = ((bf16[128,2,100,128]{3,1,2,0:T(2,128)(2,1)}), bf16[128,2,100,128]{3,1,2,0:T(2,128)(2,1)}, u32[]{:S(2)}, u32[]{:S(2)}) async-start(bf16[128,2,100,128]{3,1,2,0:T(2,128)(2,1)} %copy.34), calls=%async_computation.2 | async-start | bytes 13107200 | tf_op jit(solution)/shard_map/all_to_all | solution.py:14
  275.1 5.7 %copy-start.4 = (bf16[100,8,128]{2,1,0:T(8,128)(2,1)S(1)}, bf16[100,8,128]{2,1,0:T(8,128)(2,1)}, u32[]{:S(2)}) copy-start(bf16[100,8,128]{2,1,0:T(8,128)(2,1)} %copy-done.3) | copy-start | bytes 614404
  420.5 89.3 %all-to-all-start.4 = ((bf16[128,2,100,128]{3,1,2,0:T(2,128)(2,1)}), bf16[128,2,100,128]{3,1,2,0:T(2,128)(2,1)}, u32[]{:S(2)}, u32[]{:S(2)}) async-start(bf16[128,2,100,128]{3,1,2,0:T(2,128)(2,1)} %copy.40), calls=%async_computation.4 | async-start | bytes 13107200 | tf_op jit(solution)/shard_map/all_to_all | solution.py:14
  525.8 1.0 copy-start
  525.8 1.1 copy-start.1
where the time goes:
time: 530 us; the launch traced here: 528 us
  waiting for transfers between devices  247 us (47%)
  local copies, waits for them, and re-layouts  122 us (23%)
  blocking collectives  82.4 us (16%)
  matrix products  35.4 us (7%)
  starting transfers between devices  33.6 us (6%)
  other arithmetic  6.64 us (1%)
    all_to_all x2, waiting for transfers between devices, back_move(): lax.all_to_all(buffer, ('ice', 'ocn'), split_axis=0, concat_axis=0, tiled...  165 us
    all_to_all x1, blocking collectives, forward_move(): lax.all_to_all(buffer, ('ice', 'ocn'), split_axis=0, concat_axis=0, tiled...  82.4 us
    all_to_all x1, waiting for transfers between devices, forward_move(): lax.all_to_all(buffer, ('ice', 'ocn'), split_axis=0, concat_axis=0, tiled...  82.1 us
    scatter x2, local copies, waits for them, and re-layouts, on_device(): jnp.zeros((devices * CAP, chans, width), jnp.bfloat16).at[place].set(prods)  35.3 us
    reshape x2, local copies, waits for them, and re-layouts, on_device(): outgoing.reshape(devices, CAP, chans, width)  20.9 us
    all_to_all x2, local copies, waits for them, and re-layouts, back_move(): lax.all_to_all(buffer, ('ice', 'ocn'), split_axis=0, concat_axis=0, tiled...  13.5 us
    all_to_all x2, local copies, waits for them, and re-layouts, forward_move(): lax.all_to_all(buffer, ('ice', 'ocn'), split_axis=0, concat_axis=0, tiled...  12.7 us
    reshape x2, local copies, waits for them, and re-layouts, on_device(): replies.reshape(devices, CAP, chans, width)  12.6 us
  transfers between devices with their start and end apart: 4, of which 3 were waited for; matrix products, arithmetic and copies ran while one was open for 9% of the time, Pallas kernels for 0%

commit v1 on v0

v1 whole, which is shorter than its diff:
```python
import functools

import jax
import jax.numpy as jnp
from jax import lax
from jax.experimental import pallas as pl
from jax.experimental.pallas import tpu as pltpu
from jax.sharding import PartitionSpec as P

MESH = pl.DeviceIdType.MESH
F32 = jnp.float32
BF16 = jnp.bfloat16
I32 = jnp.int32

ROWS = (32, 32, 40)
BASE = (0, 32, 64)
CH = 104
NBLK = 128
TILES = 8
W = 128
DENSE = 128
ORDER = ((0, 1, 2), (1, 2, 0), (2, 0, 1))


def layout(cap):
    names = {}
    at = 0
    for part in range(3):
        for name, size in (
            ("perm", 8 * cap), ("keep", 8 * cap), ("last", DENSE),
            ("want", 8 * cap), ("blk", 8 * cap), ("slot", NBLK),
        ):
            names[name, part] = at
            at += size
    for name, size in (("src", NBLK), ("order", NBLK), ("same", NBLK), ("end", TILES), ("valid", NBLK)):
        names[name] = at
        at += size
    return names, at


def split(owner):
    ice, ocn = owner // 16, owner % 16
    return (ice // 2, ocn % 4, ocn // 4), ice % 2


def ranks(key):
    n = key.shape[0]
    where = jnp.arange(n, dtype=I32)
    before = (key[None, :] < key[:, None]) | ((key[None, :] == key[:, None]) & (where[None, :] < where[:, None]))
    rank = jnp.sum(before.astype(I32), axis=1)
    hit = rank[None, :] == where[:, None]
    perm = jnp.sum(jnp.where(hit, where[None, :], 0), axis=1)
    ordered = jnp.sum(jnp.where(hit, key[None, :], 0), axis=1)
    same = jnp.concatenate([jnp.zeros((1,), I32), (ordered[1:] == ordered[:-1]).astype(I32)])
    return perm, same


def ends(key, count, none):
    tile = jnp.arange(count, dtype=I32)
    upto = jnp.sum((key[None, :] <= tile[:, None]).astype(I32), axis=1) - 1
    any_ = jnp.sum((key[None, :] == tile[:, None]).astype(I32), axis=1) > 0
    return jnp.where(any_, upto, none)


def tables(cap, route, source, target, valid):
    me_ice, me_ocn = lax.axis_index("ice"), lax.axis_index("ocn")
    own = route * TILES + target
    every = lax.all_gather(own, ("ice", "ocn")).reshape(4, 2, 4, 4, NBLK)
    mine, my_core = split(me_ice * 16 + me_ocn)
    my_x, my_y, my_z = mine
    order = jnp.arange(NBLK, dtype=I32)
    pieces = []
    for part in range(3):
        first, second, third = ORDER[part]
        if part == 0:
            group = lax.dynamic_slice(every, (0, 0, my_z, my_y, 0), (4, 2, 1, 1, NBLK)).reshape(8, NBLK)
        elif part == 1:
            group = lax.dynamic_slice(every, (my_x, 0, my_z, 0, 0), (1, 2, 1, 4, NBLK)).reshape(2, 4, NBLK)
            group = jnp.transpose(group, (1, 0, 2)).reshape(8, NBLK)
        else:
            group = lax.dynamic_slice(every, (my_x, 0, 0, my_y, 0), (1, 2, 4, 1, NBLK)).reshape(2, 4, NBLK)
            group = jnp.transpose(group, (1, 0, 2)).reshape(8, NBLK)
        place, core = split(group // TILES)
        picked = (place[first] == mine[first]) & (core == my_core)
        dense = place[second] * 32 + place[third] * 8 + group % TILES
        earlier = order[None, :] < order[:, None]
        pos = jnp.sum((picked[:, None, :] & earlier[None]).astype(I32), axis=2)
        hit = picked[:, None, :] & (pos[:, None, :] == jnp.arange(cap, dtype=I32)[None, :, None])
        want = jnp.sum(jnp.where(hit, dense[:, None, :] + 1, 0), axis=2).reshape(8 * cap) - 1
        key = jnp.where(want < 0, 1000, want)
        perm, keep = ranks(key)
        last = ends(key, DENSE, 8 * cap)
        place, core = split(own // TILES)
        member = place[first] * 2 + core
        pos = jnp.sum(((member[None, :] == member[:, None]) & earlier).astype(I32), axis=1)
        slot = member * cap + pos
        hit = slot[None, :] == jnp.arange(8 * cap, dtype=I32)[:, None]
        blk = jnp.sum(jnp.where(hit, order[None, :], 0), axis=1)
        pieces += [perm, keep, last, jnp.maximum(want, 0), blk, slot]
    by_source, same = ranks(source)
    pieces += [source, by_source, same, ends(source, TILES, NBLK), valid]
    return jnp.concatenate(pieces)


def wait_in(ref, sem):
    pltpu.make_async_copy(ref, ref, sem).wait()


def body(cap, meta, ice_in, ocean, mask, rate, weights, ice_out, flux_out, ice_t, prod, pre, *rest):
    rest = list(rest)

    def take(count):
        out = rest[:count]
        del rest[:count]
        return out

    out_buf, in_buf, relay, back, back_relay = take(3), take(3), take(3), take(3), take(3)
    scan, dense, wide, rs1, rs2, rs3, rs4 = take(3), take(3), take(3), take(3), take(3), take(3), take(3)
    a_send, a_recv, r_send, r_recv, g_send, g_recv = rest
    names, unused = layout(cap)
    my_ice, my_ocn = lax.axis_index("ice"), lax.axis_index("ocn")
    x, core = my_ice // 2, my_ice % 2
    spot = (x, my_ocn % 4, my_ocn // 4)

    def device(axis, step, which):
        place = list(spot)
        place[axis] = (place[axis] + step + 4) % 4
        return (place[0] * 2 + which, place[2] * 4 + place[1])

    def push(src, dst, send, recv, to):
        copy = pltpu.make_async_remote_copy(src, dst, send, recv, device_id=to, device_id_type=MESH)
        copy.start()
        return copy

    barrier = pltpu.get_barrier_semaphore()
    peers = [(my_ice // 2 * 2 + 1 - core, my_ocn)]
    for axis in range(3):
        for step in (1, -1):
            peers += [device(axis, step, 0), device(axis, step, 1)]
    for peer in peers:
        pl.semaphore_signal(barrier, inc=1, device_id=peer, device_id_type=MESH)

    for tile in range(TILES):
        lanes = slice(tile * W, (tile + 1) * W)
        ice_t[tile] = (ice_in[:, lanes].astype(F32) * mask[:, lanes]).astype(BF16)
    for part in range(3):
        scan[part][8 * cap] = jnp.zeros((ROWS[part], W), BF16)
    pre[NBLK] = jnp.zeros((CH, W), F32)
    lane = lax.broadcasted_iota(I32, (CH, W), 1)
    pl.semaphore_wait(barrier, len(peers))

    def exchange(way, fill, into, hop):
        copies = []
        for part in range(3):
            axis = ORDER[part][0]
            q = spot[axis]
            for side, step in ((0, 1), (1, -1)):
                member = (q + 2) % 4 * 2 + side
                fill(part, member, out_buf[part], member)
                copies.append(push(
                    out_buf[part].at[pl.ds(member * cap, cap)], hop[part].at[side],
                    a_send.at[way, part, side], a_recv.at[way, part, 8 + side], device(axis, step, core)))
        for part in range(3):
            axis = ORDER[part][0]
            q = spot[axis]
            me = q * 2 + core
            for turn, (step, which) in enumerate(((1, 0), (-1, 0), (1, 1), (-1, 1))):
                member = (q + step + 4) % 4 * 2 + which
                fill(part, member, out_buf[part], member)
                copies.append(push(
                    out_buf[part].at[pl.ds(member * cap, cap)], into[part].at[pl.ds(me * cap, cap)],
                    a_send.at[way, part, 2 + turn], a_recv.at[way, part, me], device(axis, step, which)))
        for part in range(3):
            axis = ORDER[part][0]
            q = spot[axis]
            me = q * 2 + core
            member = q * 2 + 1 - core
            fill(part, member, out_buf[part], member)
            copies.append(push(
                out_buf[part].at[pl.ds(member * cap, cap)], into[part].at[pl.ds(me * cap, cap)],
                a_send.at[way, part, 6], a_recv.at[way, part, me], device(axis, 0, 1 - core)))
            fill(part, me, into[part], me)
        for part in range(3):
            axis = ORDER[part][0]
            q = spot[axis]
            for side, step in ((0, 1), (1, -1)):
                wait_in(hop[part].at[side], a_recv.at[way, part, 8 + side])
                origin = (q - step + 4) % 4 * 2 + core
                copies.append(push(
                    hop[part].at[side], into[part].at[pl.ds(origin * cap, cap)],
                    a_send.at[way, part, 7 + side], a_recv.at[way, part, origin], device(axis, step, side)))
        return copies

    def arrive(way, part, into):
        q = spot[ORDER[part][0]]
        for other in range(1, 8):
            member = (q * 2 + core + other) % 8
            wait_in(into[part].at[pl.ds(member * cap, cap)], a_recv.at[way, part, member])

    def scatter_start(part, level, ref, n, one, two):
        axis = ORDER[part][1 + level]
        q, half = spot[axis], n // 2
        send, recv = r_send.at[part, level], r_recv.at[part, level]
        far, up, down = (q + 2) % 4 * n, (q + 1) % 4 * n, (q + 3) % 4 * n
        there, here = device(axis, 1, core), device(axis, -1, core)
        return [
            push(ref.at[pl.ds(far, half)], one.at[0], send.at[0], recv.at[0], there),
            push(ref.at[pl.ds(far + half, half)], one.at[1], send.at[1], recv.at[1], here),
            push(ref.at[pl.ds(up + half, half)], two.at[0, pl.ds(half, half)], send.at[2], recv.at[2], there),
            push(ref.at[pl.ds(down, half)], two.at[1, pl.ds(0, half)], send.at[3], recv.at[3], here),
        ]

    def scatter_next(part, level, ref, n, one, two):
        axis = ORDER[part][1 + level]
        q, half = spot[axis], n // 2
        send, recv = r_send.at[part, level], r_recv.at[part, level]
        up, down = (q + 1) % 4 * n, (q + 3) % 4 * n
        there, here = device(axis, 1, core), device(axis, -1, core)
        wait_in(one.at[0], recv.at[0])
        near = pl.ds(up, half)
        ref[near] = (ref[near].astype(F32) + one[0].astype(F32)).astype(BF16)
        first = push(ref.at[near], two.at[0, pl.ds(0, half)], send.at[4], recv.at[4], there)
        wait_in(one.at[1], recv.at[1])
        near = pl.ds(down + half, half)
        ref[near] = (ref[near].astype(F32) + one[1].astype(F32)).astype(BF16)
        return [first, push(ref.at[near], two.at[1, pl.ds(half, half)], send.at[5], recv.at[5], here)]

    def scatter_end(part, level, ref, n, two):
        half = n // 2
        recv = r_recv.at[part, level]
        wait_in(two.at[0, pl.ds(half, half)], recv.at[2])
        wait_in(two.at[1, pl.ds(0, half)], recv.at[3])
        wait_in(two.at[0, pl.ds(0, half)], recv.at[4])
        wait_in(two.at[1, pl.ds(half, half)], recv.at[5])
        q = spot[ORDER[part][1 + level]]
        return ref[pl.ds(q * n, n)].astype(F32) + two[0].astype(F32) + two[1].astype(F32)

    def gather_start(part, level, n, at):
        axis = ORDER[part][1 + level]
        q, ref = spot[axis], wide[part]
        send, recv = g_send.at[part, level], g_recv.at[part, level]
        own = ref.at[pl.ds(at + q * n, n)]
        return [
            push(own, own, send.at[0], recv.at[0], device(axis, 1, core)),
            push(own, own, send.at[1], recv.at[1], device(axis, -1, core)),
        ]

    def gather_next(part, level, n, at):
        axis = ORDER[part][1 + level]
        q, ref, half = spot[axis], wide[part], n // 2
        send, recv = g_send.at[part, level], g_recv.at[part, level]
        low, high = at + (q + 3) % 4 * n, at + (q + 1) % 4 * n
        wait_in(ref.at[pl.ds(low, n)], recv.at[0])
        piece = ref.at[pl.ds(low, half)]
        first = push(piece, piece, send.at[2], recv.at[2], device(axis, 1, core))
        wait_in(ref.at[pl.ds(high, n)], recv.at[1])
        piece = ref.at[pl.ds(high + half, half)]
        return [first, push(piece, piece, send.at[3], recv.at[3], device(axis, -1, core))]

    def gather_end(part, level, n, at):
        q, ref, half = spot[ORDER[part][1 + level]], wide[part], n // 2
        recv = g_recv.at[part, level]
        far = at + (q + 2) % 4 * n
        wait_in(ref.at[pl.ds(far, half)], recv.at[2])
        wait_in(ref.at[pl.ds(far + half, half)], recv.at[3])

    def drain(copies):
        for copy in copies:
            copy.wait_send()

    def step(turn, carry):
        del turn

        def product(group, carry):
            for one in range(4):
                b = group * 4 + one
                tile = ice_t[meta[names["src"] + b]]
                tile = jnp.where(lane < meta[names["valid"] + b], tile, jnp.zeros((), BF16))
                prod[b] = jnp.dot(tile, weights[b], preferred_element_type=F32).astype(BF16)
            return carry

        lax.fori_loop(0, NBLK // 4, product, 0)

        def fill_products(part, member, ref, to):
            def put(k, carry):
                b = meta[names["blk", part] + member * cap + k]
                ref[to * cap + k] = prod[b, pl.ds(BASE[part], ROWS[part])]
                return carry

            lax.fori_loop(0, cap, put, 0, unroll=4)

        sent = exchange(0, fill_products, in_buf, relay)
        level0, level1 = [], []
        for part in range(3):
            arrive(0, part, in_buf)

            def add(group, acc, part=part):
                for one in range(4):
                    r = group * 4 + one
                    piece = in_buf[part][meta[names["perm", part] + r]].astype(F32)
                    acc = acc * meta[names["keep", part] + r].astype(F32) + piece
                    scan[part][r] = acc.astype(BF16)
                return acc

            lax.fori_loop(0, 2 * cap, add, jnp.zeros((ROWS[part], W), F32))

            def settle(t, carry, part=part):
                dense[part][t] = scan[part][meta[names["last", part] + t]]
                return carry

            lax.fori_loop(0, DENSE, settle, 0, unroll=8)
            level0 += scatter_start(part, 0, dense[part], 32, rs1[part], rs2[part])
        drain(sent)
        for part in range(3):
            level0 += scatter_next(part, 0, dense[part], 32, rs1[part], rs2[part])
        for part in range(3):
            q = spot[ORDER[part][1]]
            total = scatter_end(part, 0, dense[part], 32, rs2[part])
            dense[part][pl.ds(q * 32, 32)] = total.astype(BF16)
            level1 += scatter_start(part, 1, dense[part].at[pl.ds(q * 32, 32)], 8, rs3[part], rs4[part])
        for part in range(3):
            q = spot[ORDER[part][1]]
            level1 += scatter_next(part, 1, dense[part].at[pl.ds(q * 32, 32)], 8, rs3[part], rs4[part])
        drain(level0)
        gather1, gather0 = [], []
        for part in range(3):
            q, p = spot[ORDER[part][1]], spot[ORDER[part][2]]
            total = scatter_end(part, 1, dense[part].at[pl.ds(q * 32, 32)], 8, rs4[part])
            rows = slice(BASE[part], BASE[part] + ROWS[part])
            for tile in range(TILES):
                lanes = slice(tile * W, (tile + 1) * W)
                flux = jnp.tanh(total[tile] + ocean[rows, lanes].astype(F32)).astype(BF16)
                flux_out[rows, lanes] = flux
                wide[part][q * 32 + p * 8 + tile] = flux
            gather1 += gather_start(part, 1, 8, q * 32)
        drain(level1)
        for part in range(3):
            gather1 += gather_next(part, 1, 8, spot[ORDER[part][1]] * 32)
        for part in range(3):
            gather_end(part, 1, 8, spot[ORDER[part][1]] * 32)
            gather0 += gather_start(part, 0, 32, 0)
        drain(gather1)
        for part in range(3):
            gather0 += gather_next(part, 0, 32, 0)
        for part in range(3):
            gather_end(part, 0, 32, 0)
        drain(gather0)

        def fill_flux(part, member, ref, to):
            def put(k, carry):
                ref[to * cap + k] = wide[part][meta[names["want", part] + member * cap + k]]
                return carry

            lax.fori_loop(0, cap, put, 0, unroll=4)

        sent = exchange(1, fill_flux, back, back_relay)
        for part in range(3):
            arrive(1, part, back)

        def force(group, acc):
            for one in range(4):
                r = group * 4 + one
                b = meta[names["order"] + r]
                taken = jnp.concatenate([back[part][meta[names["slot", part] + b]] for part in range(3)], axis=0)
                term = lax.dot_general(taken, weights[b], (((1,), (1,)), ((), ())), preferred_element_type=F32)
                term = jnp.where(lane < meta[names["valid"] + b], term, 0.0)
                acc = acc * meta[names["same"] + r].astype(F32) + term
                pre[r] = acc
            return acc

        lax.fori_loop(0, NBLK // 4, force, jnp.zeros((CH, W), F32))
        for tile in range(TILES):
            lanes = slice(tile * W, (tile + 1) * W)
            forcing = pre[meta[names["end"] + tile]]
            new = (mask[:, lanes] * (ice_t[tile].astype(F32) + rate[...] * jnp.tanh(forcing))).astype(BF16)
            ice_t[tile] = new
            ice_out[:, lanes] = new
        drain(sent)
        return carry

    lax.fori_loop(0, 2, step, 0)


def couple(cap, meta, ice, ocean, mask, rate, weights):
    cells = TILES * W
    scratch = [pltpu.VMEM((TILES, CH, W), BF16), pltpu.VMEM((NBLK, CH, W), BF16), pltpu.VMEM((NBLK + 1, CH, W), F32)]
    for shape in (
        (8 * cap,), (8 * cap,), (2, cap), (8 * cap,), (2, cap), (8 * cap + 1,), (DENSE,), (DENSE,),
        (2, 16), (2, 32), (2, 4), (2, 8),
    ):
        scratch += [pltpu.VMEM(shape + (rows, W), BF16) for rows in ROWS]
    scratch += [
        pltpu.SemaphoreType.DMA((2, 3, 9)), pltpu.SemaphoreType.DMA((2, 3, 10)),
        pltpu.SemaphoreType.DMA((3, 2, 6)), pltpu.SemaphoreType.DMA((3, 2, 6)),
        pltpu.SemaphoreType.DMA((3, 2, 4)), pltpu.SemaphoreType.DMA((3, 2, 4)),
    ]
    vmem = pl.BlockSpec(memory_space=pltpu.VMEM)
    return pl.pallas_call(
        functools.partial(body, cap),
        out_shape=(jax.ShapeDtypeStruct((CH, cells), BF16), jax.ShapeDtypeStruct((CH, cells), BF16)),
        in_specs=[pl.BlockSpec(memory_space=pltpu.SMEM)] + [vmem] * 5,
        out_specs=(vmem, vmem),
        scratch_shapes=scratch,
        compiler_params=pltpu.CompilerParams(
            collective_id=0, has_side_effects=True, vmem_limit_bytes=66 * 1024 * 1024 - 2200000
        ),
    )(meta, ice, ocean, mask, rate, weights)


def on_device(ice_state, ocean_state, ice_rate, block_weights, block_route, block_tiles, block_valid, ice_mask):
    cats, fields, cells = ice_state.shape
    chans = cats * fields
    cap = 32
    meta = tables(cap, block_route[:, 0], block_tiles[:, 0], block_tiles[:, 1], block_valid)
    grow = ((0, CH - chans), (0, 0))
    ice = jnp.pad(ice_state.reshape(chans, cells), grow)
    ocean = jnp.pad(ocean_state.reshape(chans, cells), grow)
    rate = jnp.pad(ice_rate.reshape(chans, 1), grow)
    mask = ice_mask.astype(F32)[None, :]
    ice, flux = couple(cap, meta, ice, ocean, mask, rate, block_weights)
    return ice[:chans].reshape(cats, fields, cells), flux[:chans].reshape(cats, fields, cells)


def solution(mesh):
    placed = (
        P(None, None, ("ice", "ocn")),
        P(None, None, ("ice", "ocn")),
        P(),
        P(("ice", "ocn"), None, None),
        P(("ice", "ocn"), None),
        P(("ice", "ocn"), None),
        P(("ice", "ocn")),
        P(("ice", "ocn")),
    )
    return jax.shard_map(
        on_device,
        mesh=mesh,
        in_specs=placed,
        out_specs=(P(None, None, ("ice", "ocn")), P(None, None, ("ice", "ocn"))),
        check_vma=False,
    )
```

time: 530 us -> 301 us (0.57)
  waiting for transfers between devices: 247 us -> 0 us
  Pallas kernels: 0 us -> 235 us
  local copies, waits for them, and re-layouts: 122 us -> 9.69 us
  blocking collectives: 82.4 us -> 46.7 us
  matrix products: 35.4 us -> 0 us
  starting transfers between devices: 33.6 us -> 0 us
    all_to_all x4 -> x0, waiting for transfers between devices: 247 us -> none  [the longest x2 165 us: back_move(): lax.all_to_all(buffer, ('ice', 'ocn'), split_axis=0, concat_axis=0, tiled...]
    pallas_call x0 -> x1, Pallas kernels: none -> 235 us  [couple(): pl.pallas_call(functools.partial(body, cap), out_shape=(jax.ShapeDtypeStr...]
    all_to_all x1 -> x0, blocking collectives: 82.4 us -> none  [forward_move(): lax.all_to_all(buffer, ('ice', 'ocn'), split_axis=0, concat_axis=0, tiled...]
    all_gather x0 -> x1, blocking collectives: none -> 46.7 us  [tables(): every = lax.all_gather(own, ('ice', 'ocn')).reshape(4, 2, 4, 4, NBLK)]
    scatter x3 -> x0, local copies, waits for them, and re-layouts: 36.3 us -> none  [the longest x2 35.3 us: on_device(): jnp.zeros((devices * CAP, chans, width), jnp.bfloat16).at[place].set(prods)]
    dot_general x9 -> x0, matrix products: 35.4 us -> none  [the longest x2 12.6 us: on_device(): jnp.einsum('cbi,bio->bco', picked, masked, preferred_element_type=jnp.flo...]
    all_to_all x4 -> x0, starting transfers between devices: 33.6 us -> none  [the longest x2 12.2 us: back_move(): lax.all_to_all(buffer, ('ice', 'ocn'), split_axis=0, concat_axis=0, tiled...]
    reshape x5, local copies, waits for them, and re-layouts: 33.6 us -> 6.06 us  [the longest x1 1.66 us: on_device(): flux[:chans].reshape(cats, fields, cells)]
  transfers between devices with their start and end apart: 4 -> 0, of which waited for: 3 -> 0; matrix products, arithmetic and copies ran while one was open for 9% -> 0% of each run, Pallas kernels for 0% -> 0%
where the time goes in v1:
time: 301 us; the launch traced here: 299 us
  Pallas kernels  235 us (78%)
  blocking collectives  46.7 us (16%)
  local copies, waits for them, and re-layouts  9.69 us (3%)
  other arithmetic  6.45 us (2%)
    pallas_call x1, Pallas kernels, couple(): pl.pallas_call(functools.partial(body, cap), out_shape=(jax.ShapeDtypeStr...  235 us
    all_gather x1, blocking collectives, tables(): every = lax.all_gather(own, ('ice', 'ocn')).reshape(4, 2, 4, 4, NBLK)  46.7 us

profile of v1, /device:TPU:0, one launch (start us, length us, event | category | flops | bytes accessed | tf_op | source)
XLA Modules:
  0.0 299.1 jit_solution(16952390855990234256)
XLA Ops:
  0.7 0.8 compare_select_fusion.17
  1.5 0.2 convert_reduce_fusion.12
  1.7 0.1 select_reduce_fusion.12
  1.8 0.1 compare_convert_fusion
  2.0 0.2 convert_reduce_fusion.13
  2.2 0.1 select_reduce_fusion.6
  2.3 0.1 convert_reduce_fusion.16
  2.4 1.3 convert_element_type.96
  3.7 0.8 reshape.726
  4.5 0.6 pad.13.rate
  5.1 46.7 %all-gather = s32[16384,1]{0,1:T(1,128)S(1)} all-gather(s32[128,1]{0,1:T(1,128)S(1)} %get-tuple-element.35), channel_id=2, replica_groups=mesh['ice'=8,'ocn'=16] {'ice','ocn'}, dimensions={0}, use_global_device_ids=true | all-gather | bytes 66048 | tf_op jit(solution)/shard_map/all_gather | solution.py:68
  52.0 0.5 convert_reduce_fusion
  52.5 0.2 select_reduce_fusion.7
  52.8 0.1 sub.149
  52.9 0.2 select_reduce_fusion.11
  53.1 0.1 sub.129
  53.2 0.2 select_reduce_fusion.9
  53.4 0.1 sub.142
  53.5 0.2 convert_reduce_fusion.4
  53.7 0.1 convert_reduce_fusion.8
  53.9 0.2 convert_reduce_fusion.5
  54.0 0.2 select_reduce_fusion.4
  54.2 0.1 compare_convert_fusion.3
  54.3 0.1 convert_reduce_fusion.10
  54.4 0.2 convert_reduce_fusion.14
  54.6 0.2 convert_reduce_fusion.15
  54.8 0.1 select_reduce_fusion.10
  54.9 0.1 select_reduce_fusion.8
  55.0 0.2 convert_reduce_fusion.3
  55.2 0.3 select_reduce_fusion
  55.5 0.1 compare_convert_fusion.1
  55.6 0.1 convert_reduce_fusion.6
  55.7 0.1 compare_convert_fusion.2
  55.8 1.3 concatenate.3.meta
  57.1 1.0 reshape.719
  58.1 0.7 pad.11.ice_in
  58.8 1.0 reshape.720
  59.8 0.7 pad.12.ocean
  60.5 235.3 %shard_map.95 = (bf16[104,1024]{1,0:T(8,128)(2,1)}, bf16[104,1024]{1,0:T(8,128)(2,1)}) custom-call(s32[4360]{0:T(1024)} %concatenate.3.meta, bf16[104,1024]{1,0:T(8,128)(2,1)} %pad.11.ice_in, bf16[104,1024]{1,0:T(8,128)(2,1)} %pad.12.ocean, f32[1,1024]{1,0:T(1,128)} %bitcast.45, f32[104,1]{1,0:T(8,128)} %pad.13.rate, bf16[128,128,128]{2,1,0:T(8,128)(2,1)} %weights.1), custom_call_target="tpu_custom_call" | custom-call | tf_op jit(solution)/shard_map/pallas_call | solution.py:398
  295.8 1.7 reshape.723
  297.4 1.7 reshape.722
  (28 shorter events, 0.4 us)

commit v2 on v1

--- a/solution.py
+++ b/solution.py
@@ -18,17 +18,19 @@
 NBLK = 128
 TILES = 8
 W = 128
+MOST = 32
+FEW = 20
 DENSE = 128
 ORDER = ((0, 1, 2), (1, 2, 0), (2, 0, 1))
 
 
-def layout(cap):
+def layout():
     names = {}
     at = 0
     for part in range(3):
         for name, size in (
-            ("perm", 8 * cap), ("keep", 8 * cap), ("last", DENSE),
-            ("want", 8 * cap), ("blk", 8 * cap), ("slot", NBLK),
+            ("perm", 8 * MOST), ("keep", 8 * MOST), ("last", DENSE),
+            ("want", 8 * MOST), ("blk", 8 * MOST), ("slot", NBLK),
         ):
             names[name, part] = at
             at += size
@@ -62,39 +64,33 @@
     return jnp.where(any_, upto, none)
 
 
-def tables(cap, route, source, target, valid):
+def tables(every, own, source, valid):
     me_ice, me_ocn = lax.axis_index("ice"), lax.axis_index("ocn")
-    own = route * TILES + target
-    every = lax.all_gather(own, ("ice", "ocn")).reshape(4, 2, 4, 4, NBLK)
+    every = every.reshape(4, 4, 4, 2, NBLK)
     mine, my_core = split(me_ice * 16 + me_ocn)
     my_x, my_y, my_z = mine
     order = jnp.arange(NBLK, dtype=I32)
     pieces = []
     for part in range(3):
         first, second, third = ORDER[part]
-        if part == 0:
-            group = lax.dynamic_slice(every, (0, 0, my_z, my_y, 0), (4, 2, 1, 1, NBLK)).reshape(8, NBLK)
-        elif part == 1:
-            group = lax.dynamic_slice(every, (my_x, 0, my_z, 0, 0), (1, 2, 1, 4, NBLK)).reshape(2, 4, NBLK)
-            group = jnp.transpose(group, (1, 0, 2)).reshape(8, NBLK)
-        else:
-            group = lax.dynamic_slice(every, (my_x, 0, 0, my_y, 0), (1, 2, 4, 1, NBLK)).reshape(2, 4, NBLK)
-            group = jnp.transpose(group, (1, 0, 2)).reshape(8, NBLK)
+        at, size = [my_z, my_y, my_x, 0, 0], [1, 1, 1, 2, NBLK]
+        at[2 - first], size[2 - first] = 0, 4
+        group = lax.dynamic_slice(every, at, size).reshape(8, NBLK)
         place, core = split(group // TILES)
         picked = (place[first] == mine[first]) & (core == my_core)
         dense = place[second] * 32 + place[third] * 8 + group % TILES
         earlier = order[None, :] < order[:, None]
         pos = jnp.sum((picked[:, None, :] & earlier[None]).astype(I32), axis=2)
-        hit = picked[:, None, :] & (pos[:, None, :] == jnp.arange(cap, dtype=I32)[None, :, None])
-        want = jnp.sum(jnp.where(hit, dense[:, None, :] + 1, 0), axis=2).reshape(8 * cap) - 1
+        hit = picked[:, None, :] & (pos[:, None, :] == jnp.arange(MOST, dtype=I32)[None, :, None])
+        want = jnp.sum(jnp.where(hit, dense[:, None, :] + 1, 0), axis=2).reshape(8 * MOST) - 1
         key = jnp.where(want < 0, 1000, want)
         perm, keep = ranks(key)
-        last = ends(key, DENSE, 8 * cap)
+        last = ends(key, DENSE, 8 * MOST)
         place, core = split(own // TILES)
         member = place[first] * 2 + core
         pos = jnp.sum(((member[None, :] == member[:, None]) & earlier).astype(I32), axis=1)
-        slot = member * cap + pos
-        hit = slot[None, :] == jnp.arange(8 * cap, dtype=I32)[:, None]
+        slot = member * MOST + pos
+        hit = slot[None, :] == jnp.arange(8 * MOST, dtype=I32)[:, None]
         blk = jnp.sum(jnp.where(hit, order[None, :], 0), axis=1)
         pieces += [perm, keep, last, jnp.maximum(want, 0), blk, slot]
     by_source, same = ranks(source)
@@ -102,6 +98,70 @@
     return jnp.concatenate(pieces)
 
 
+def most(every):
+    place, core = split(every.reshape(NBLK, NBLK) // TILES)
+    member = jnp.stack([place[axis] * 2 + core for axis in range(3)])
+    hit = member[:, :, None, :] == jnp.arange(8, dtype=I32)[None, None, :, None]
+    return jnp.max(jnp.sum(hit.astype(I32), axis=3))
+
+
+def spread(own, every, send, recv):
+    my_ice, my_ocn = lax.axis_index("ice"), lax.axis_index("ocn")
+    y, z = my_ocn % 4, my_ocn // 4
+
+    def near(k):
+        return ((my_ice + k) % 8, my_ocn)
+
+    def along_y(k):
+        return (my_ice, z * 4 + (y + k) % 4)
+
+    def along_z(k):
+        return (my_ice, (z + k) % 4 * 4 + y)
+
+    peers = [near(k) for k in range(1, 8)] + [along_y(k) for k in range(1, 4)] + [along_z(k) for k in range(1, 4)]
+    barrier = pltpu.get_barrier_semaphore()
+    for peer in peers:
+        pl.semaphore_signal(barrier, inc=1, device_id=peer, device_id_type=MESH)
+    line = my_ocn * 8
+    every[line + my_ice] = own[...]
+    pl.semaphore_wait(barrier, len(peers))
+
+    def level(base, count, first, rows, to, mine):
+        piece = every.at[pl.ds(first, rows)]
+        copies = []
+        for k in range(1, count):
+            copies.append(pltpu.make_async_remote_copy(
+                piece, piece, send.at[base + k], recv.at[base + mine], device_id=to(k), device_id_type=MESH))
+            copies[-1].start()
+        return copies
+
+    def gathered(base, count, mine, where, rows):
+        for k in range(1, count):
+            other = (mine + k) % count
+            wait_in(every.at[pl.ds(where(other), rows)], recv.at[base + other])
+
+    sent = level(0, 8, line + my_ice, 1, near, my_ice)
+    gathered(0, 8, my_ice, lambda k: line + k, 1)
+    sent += level(8, 4, line, 8, along_y, y)
+    gathered(8, 4, y, lambda k: (z * 4 + k) * 8, 8)
+    sent += level(12, 4, z * 32, 32, along_z, z)
+    gathered(12, 4, z, lambda k: k * 32, 32)
+    for copy in sent:
+        copy.wait_send()
+
+
+def everyone(own):
+    vmem = pl.BlockSpec(memory_space=pltpu.VMEM)
+    return pl.pallas_call(
+        spread,
+        out_shape=jax.ShapeDtypeStruct((NBLK, 1, NBLK), I32),
+        in_specs=[vmem],
+        out_specs=vmem,
+        scratch_shapes=[pltpu.SemaphoreType.DMA((16,)), pltpu.SemaphoreType.DMA((16,))],
+        compiler_params=pltpu.CompilerParams(collective_id=0, has_side_effects=True),
+    )(own.reshape(1, NBLK))
+
+
 def wait_in(ref, sem):
     pltpu.make_async_copy(ref, ref, sem).wait()
 
@@ -117,7 +177,7 @@
     out_buf, in_buf, relay, back, back_relay = take(3), take(3), take(3), take(3), take(3)
     scan, dense, wide, rs1, rs2, rs3, rs4 = take(3), take(3), take(3), take(3), take(3), take(3), take(3)
     a_send, a_recv, r_send, r_recv, g_send, g_recv = rest
-    names, unused = layout(cap)
+    names, unused = layout()
     my_ice, my_ocn = lax.axis_index("ice"), lax.axis_index("ocn")
     x, core = my_ice // 2, my_ice % 2
     spot = (x, my_ocn % 4, my_ocn // 4)
@@ -144,7 +204,7 @@
         lanes = slice(tile * W, (tile + 1) * W)
         ice_t[tile] = (ice_in[:, lanes].astype(F32) * mask[:, lanes]).astype(BF16)
     for part in range(3):
-        scan[part][8 * cap] = jnp.zeros((ROWS[part], W), BF16)
+        scan[part][8 * MOST] = jnp.zeros((ROWS[part], W), BF16)
     pre[NBLK] = jnp.zeros((CH, W), F32)
     lane = lax.broadcasted_iota(I32, (CH, W), 1)
     pl.semaphore_wait(barrier, len(peers))
@@ -158,7 +218,7 @@
                 member = (q + 2) % 4 * 2 + side
                 fill(part, member, out_buf[part], member)
                 copies.append(push(
-                    out_buf[part].at[pl.ds(member * cap, cap)], hop[part].at[side],
+                    out_buf[part].at[pl.ds(member * MOST, cap)], hop[part].at[side],
                     a_send.at[way, part, side], a_recv.at[way, part, 8 + side], device(axis, step, core)))
         for part in range(3):
             axis = ORDER[part][0]
@@ -168,7 +228,7 @@
                 member = (q + step + 4) % 4 * 2 + which
                 fill(part, member, out_buf[part], member)
                 copies.append(push(
-                    out_buf[part].at[pl.ds(member * cap, cap)], into[part].at[pl.ds(me * cap, cap)],
+                    out_buf[part].at[pl.ds(member * MOST, cap)], into[part].at[pl.ds(me * MOST, cap)],
                     a_send.at[way, part, 2 + turn], a_recv.at[way, part, me], device(axis, step, which)))
         for part in range(3):
             axis = ORDER[part][0]
@@ -177,7 +237,7 @@
             member = q * 2 + 1 - core
             fill(part, member, out_buf[part], member)
             copies.append(push(
-                out_buf[part].at[pl.ds(member * cap, cap)], into[part].at[pl.ds(me * cap, cap)],
+                out_buf[part].at[pl.ds(member * MOST, cap)], into[part].at[pl.ds(me * MOST, cap)],
                 a_send.at[way, part, 6], a_recv.at[way, part, me], device(axis, 0, 1 - core)))
             fill(part, me, into[part], me)
         for part in range(3):
@@ -187,7 +247,7 @@
                 wait_in(hop[part].at[side], a_recv.at[way, part, 8 + side])
                 origin = (q - step + 4) % 4 * 2 + core
                 copies.append(push(
-                    hop[part].at[side], into[part].at[pl.ds(origin * cap, cap)],
+                    hop[part].at[side], into[part].at[pl.ds(origin * MOST, cap)],
                     a_send.at[way, part, 7 + side], a_recv.at[way, part, origin], device(axis, step, side)))
         return copies
 
@@ -195,7 +255,7 @@
         q = spot[ORDER[part][0]]
         for other in range(1, 8):
             member = (q * 2 + core + other) % 8
-            wait_in(into[part].at[pl.ds(member * cap, cap)], a_recv.at[way, part, member])
+            wait_in(into[part].at[pl.ds(member * MOST, cap)], a_recv.at[way, part, member])
 
     def scatter_start(part, level, ref, n, one, two):
         axis = ORDER[part][1 + level]
@@ -283,8 +343,8 @@
 
         def fill_products(part, member, ref, to):
             def put(k, carry):
-                b = meta[names["blk", part] + member * cap + k]
-                ref[to * cap + k] = prod[b, pl.ds(BASE[part], ROWS[part])]
+                b = meta[names["blk", part] + member * MOST + k]
+                ref[to * MOST + k] = prod[b, pl.ds(BASE[part], ROWS[part])]
                 return carry
 
             lax.fori_loop(0, cap, put, 0, unroll=4)
@@ -348,7 +408,7 @@
 
         def fill_flux(part, member, ref, to):
             def put(k, carry):
-                ref[to * cap + k] = wide[part][meta[names["want", part] + member * cap + k]]
+                ref[to * MOST + k] = wide[part][meta[names["want", part] + member * MOST + k]]
                 return carry
 
             lax.fori_loop(0, cap, put, 0, unroll=4)
@@ -381,11 +441,11 @@
     lax.fori_loop(0, 2, step, 0)
 
 
-def couple(cap, meta, ice, ocean, mask, rate, weights):
+def couple(cap, which, meta, ice, ocean, mask, rate, weights):
     cells = TILES * W
     scratch = [pltpu.VMEM((TILES, CH, W), BF16), pltpu.VMEM((NBLK, CH, W), BF16), pltpu.VMEM((NBLK + 1, CH, W), F32)]
     for shape in (
-        (8 * cap,), (8 * cap,), (2, cap), (8 * cap,), (2, cap), (8 * cap + 1,), (DENSE,), (DENSE,),
+        (8 * MOST,), (8 * MOST,), (2, cap), (8 * MOST,), (2, cap), (8 * MOST + 1,), (DENSE,), (DENSE,),
         (2, 16), (2, 32), (2, 4), (2, 8),
     ):
         scratch += [pltpu.VMEM(shape + (rows, W), BF16) for rows in ROWS]
@@ -402,7 +462,7 @@
         out_specs=(vmem, vmem),
         scratch_shapes=scratch,
         compiler_params=pltpu.CompilerParams(
-            collective_id=0, has_side_effects=True, vmem_limit_bytes=66 * 1024 * 1024 - 2200000
+            collective_id=which, has_side_effects=True, vmem_limit_bytes=66 * 1024 * 1024 - 2200000
         ),
     )(meta, ice, ocean, mask, rate, weights)
 
@@ -410,14 +470,20 @@
 def on_device(ice_state, ocean_state, ice_rate, block_weights, block_route, block_tiles, block_valid, ice_mask):
     cats, fields, cells = ice_state.shape
     chans = cats * fields
-    cap = 32
-    meta = tables(cap, block_route[:, 0], block_tiles[:, 0], block_tiles[:, 1], block_valid)
+    own = block_route[:, 0] * TILES + block_tiles[:, 1]
+    every = everyone(own)
+    meta = tables(every, own, block_tiles[:, 0], block_valid)
     grow = ((0, CH - chans), (0, 0))
     ice = jnp.pad(ice_state.reshape(chans, cells), grow)
     ocean = jnp.pad(ocean_state.reshape(chans, cells), grow)
     rate = jnp.pad(ice_rate.reshape(chans, 1), grow)
     mask = ice_mask.astype(F32)[None, :]
-    ice, flux = couple(cap, meta, ice, ocean, mask, rate, block_weights)
+    ice, flux = lax.cond(
+        most(every) <= FEW,
+        functools.partial(couple, FEW, 1),
+        functools.partial(couple, MOST, 2),
+        meta, ice, ocean, mask, rate, block_weights,
+    )
     return ice[:chans].reshape(cats, fields, cells), flux[:chans].reshape(cats, fields, cells)
 
 

time: 301 us -> 237 us (0.79)
  blocking collectives: 46.7 us -> 0 us
  Pallas kernels: 235 us -> 209 us
  other arithmetic: 6.45 us -> 16.3 us
    all_gather x1 -> x0, blocking collectives: 46.7 us -> none  [tables(): every = lax.all_gather(own, ('ice', 'ocn')).reshape(4, 2, 4, 4, NBLK)]
    pallas_call x1, Pallas kernels: 235 us -> 191 us  [couple(): pl.pallas_call(functools.partial(body, cap), out_shape=(jax.ShapeDtypeStr...]
    pallas_call x0 -> x1, Pallas kernels: none -> 18.6 us  [everyone(): pl.pallas_call(spread, out_shape=jax.ShapeDtypeStruct((NBLK, 1, NBLK), I3...]
    reduce_sum x3 -> x4, other arithmetic: 0.63 us -> 7.18 us  [the longest x1 6.54 us: most(): return jnp.max(jnp.sum(hit.astype(I32), axis=3))]
where the time goes in v2:
time: 237 us; the launch traced here: 236 us
  Pallas kernels  209 us (88%)
  other arithmetic  16.3 us (7%)
  local copies, waits for them, and re-layouts  8.59 us (4%)
    pallas_call x1, Pallas kernels, couple(): pl.pallas_call(functools.partial(body, cap), out_shape=(jax.ShapeDtypeStr...  191 us
    pallas_call x1, Pallas kernels, everyone(): pl.pallas_call(spread, out_shape=jax.ShapeDtypeStruct((NBLK, 1, NBLK), I3...  18.6 us
    reduce_sum x1, other arithmetic, most(): return jnp.max(jnp.sum(hit.astype(I32), axis=3))  6.54 us

profile of v2, /device:TPU:0, one launch (start us, length us, event | category | flops | bytes accessed | tf_op | source)
XLA Modules:
  0.0 235.8 jit_solution(1712811818330873136)
XLA Ops:
  0.8 1.3 compare_select_fusion.17
  2.1 0.2 convert_reduce_fusion.13
  2.3 0.1 select_reduce_fusion.12
  2.4 0.1 compare_convert_fusion
  2.5 0.1 convert_reduce_fusion.17
  2.7 0.7 convert_element_type.82
  3.4 18.6 %shard_map.95 = s32[128,1,128]{2,1,0:T(1,128)} custom-call(s32[1,128]{1,0:T(1,128)} %bitcast.67), custom_call_target="tpu_custom_call" | custom-call | tf_op jit(solution)/shard_map/pallas_call | solution.py:155
  21.9 0.7 constant_dynamic-slice_fusion
  22.7 0.7 constant_dynamic-slice_fusion.1
  23.5 0.7 constant_dynamic-slice_fusion.2
  24.2 0.5 convert_reduce_fusion.1
  24.7 0.2 select_reduce_fusion.9
  24.9 0.2 select_reduce_fusion.7
  25.1 0.1 sub.171
  25.2 0.1 sub.164
  25.3 0.2 select_reduce_fusion.11
  25.5 0.1 sub.151
  25.6 0.2 convert_reduce_fusion.6
  25.8 0.2 select_reduce_fusion.4
  26.0 0.1 compare_convert_fusion.3
  26.1 0.1 convert_reduce_fusion.11
  26.2 0.7 compare_select_fusion.26
  26.9 0.2 convert_reduce_fusion.14
  27.1 0.2 convert_reduce_fusion.15
  27.3 0.2 convert_reduce_fusion.16
  27.4 0.1 select_reduce_fusion.10
  27.6 0.1 select_reduce_fusion.8
  27.7 0.1 select_reduce_fusion.6
  27.8 0.2 convert_reduce_fusion.5
  28.0 0.1 convert_reduce_fusion.9
  28.1 0.2 convert_reduce_fusion.4
  28.3 0.3 select_reduce_fusion
  28.6 0.1 compare_convert_fusion.1
  28.7 0.1 convert_reduce_fusion.7
  28.8 0.1 compare_convert_fusion.2
  28.9 0.7 concatenate.3
  29.6 1.0 fusion.11
  30.6 1.0 fusion.13
  31.6 6.5 %convert_reduce_fusion = s32[3,128,8]{2,1,0:T(8,128)S(1)} fusion(s32[3,128,128]{2,1,0:T(8,128)S(1)} %pad_add_fusion), kind=kLoop, calls=%fused_computation | loop fusion | flops 1176576 | bytes 208896 | tf_op jit(solution)/shard_map/reduce_sum | solution.py:105
  38.2 0.7 reduce_max.9
  39.5 192.9 %conditional.1 = ((bf16[104,1024]{1,0:T(8,128)(2,1)}, bf16[104,1024]{1,0:T(8,128)(2,1)})) conditional(s32[]{:T(128)} %convert_element_type.81, (bf16[5,20,1024]{2,1,0:T(8,128)(2,1)S(1)}, bf16[5,20,1024]{2,1,0:T(8,128)(2,1)S(1)}, f32[1024]{0:T(1024)S(1)}, f32[5,20]{1,0:T(8,128)S(1)}, s32[4360]{0:T(1024)S(1)}, ...), branch_computations={%region_34.35_spmd, %region_35.36_spmd} | conditional | bytes 1656416 | solution.py:481
  39.7 0.1 reshape.1056
  39.8 0.6 pad.28.rate
  40.5 0.7 pad.26.ice_in
  41.2 0.7 pad.27.ocean
  42.0 190.5 %branch_1_fun.2 = (bf16[104,1024]{1,0:T(8,128)(2,1)}, bf16[104,1024]{1,0:T(8,128)(2,1)}) custom-call(s32[4360]{0:T(1024)S(1)} %get-tuple-element.88.meta, bf16[104,1024]{1,0:T(8,128)(2,1)} %pad.26.ice_in, bf16[104,1024]{1,0:T(8,128)(2,1)} %pad.27.ocean, f32[1,1024]{1,0:T(1,128)S(1)} %bitcast.66, f32[104,1]{1,0:T(8,128)} %pad.28.rate, ...), custom_call_target="tpu_custom_call" | custom-call | tf_op jit(solution)/shard_map/cond/branch_1_fun/pallas_call | solution.py:458
  232.5 1.7 reshape.1054
  234.2 1.7 reshape.1053
  (31 shorter events, 0.4 us)
Async XLA Ops:
  0.6 38.9 %copy-start.2 = (f32[5,20]{1,0:T(8,128)S(1)}, f32[5,20]{1,0:T(8,128)}, u32[]{:S(2)}) copy-start(f32[5,20]{1,0:T(8,128)} %param.12) | copy-start | bytes 1204
  0.6 38.9 %copy-start.1 = (bf16[5,20,1024]{2,1,0:T(8,128)(2,1)S(1)}, bf16[5,20,1024]{2,1,0:T(8,128)(2,1)}, u32[]{:S(2)}) copy-start(bf16[5,20,1024]{2,1,0:T(8,128)(2,1)} %param.11) | copy-start | bytes 614404
  0.7 38.9 %copy-start = (bf16[5,20,1024]{2,1,0:T(8,128)(2,1)S(1)}, bf16[5,20,1024]{2,1,0:T(8,128)(2,1)}, u32[]{:S(2)}) copy-start(bf16[5,20,1024]{2,1,0:T(8,128)(2,1)} %param.10) | copy-start | bytes 614404

commit v3 on v0

v3 whole, which is shorter than its diff:
```python
import functools

import jax
import jax.numpy as jnp
from jax import lax
from jax.experimental import pallas as pl
from jax.experimental.pallas import tpu as pltpu
from jax.sharding import PartitionSpec as P

MESH = pl.DeviceIdType.MESH
F32 = jnp.float32
BF16 = jnp.bfloat16
I32 = jnp.int32

ROWS = (32, 32, 40)
HALVES = ((16, 16, 16), (16, 16, 24))
LEAD = 1
PLAN = (0,) * LEAD + (0, 1) * 40
LISTEN = 1
CH = 104
NBLK = 128
TILES = 8
W = 128
MOST = 32
FEW = 20
DENSE = 128
ORDER = ((0, 1, 2), (1, 2, 0), (2, 0, 1))


def split(owner):
    ice, ocn = owner >> 4, owner & 15
    return (ice >> 1, ocn & 3, ocn >> 2), ice & 1


def at_row(shape):
    return lax.broadcasted_iota(I32, shape, 0)


def at_lane(shape):
    return lax.broadcasted_iota(I32, shape, 1)


def down(values, keep):
    return jnp.sum(jnp.where(keep, values, 0), axis=0, keepdims=True)


def across(values, keep):
    return jnp.sum(jnp.where(keep, values, 0), axis=1, keepdims=True)


def column(row):
    n = row.shape[1]
    return across(row, at_row((n, n)) == at_lane((n, n)))


def line(col):
    n = col.shape[0]
    return down(col, at_row((n, n)) == at_lane((n, n)))


def sort_tables(key_row, key_col, count, none):
    n = key_row.shape[1]
    wide_row, wide_col = at_lane((n, n)), at_row((n, n))
    before = key_row * n + at_lane((1, n)) < key_col * n + at_row((n, 1))
    rank = across(1, before)
    hit = rank == wide_row
    perm = down(wide_col, hit)
    ordered = down(key_col, hit)
    earlier = down(key_col, rank + 1 == wide_row)
    same = jnp.where((ordered == earlier) & (at_lane((1, n)) > 0), 1, 0)
    tile = at_lane((n, W))
    upto = down(1, jnp.broadcast_to(key_col <= tile, (n, W))) - 1
    found = down(1, jnp.broadcast_to(key_col == tile, (n, W)))
    return perm, same, jnp.where(found > 0, upto, none)


def own_tables(goal, source):
    goal_col = column(goal)
    rows, most = [], jnp.zeros((1, NBLK), I32)
    earlier = at_row((NBLK, NBLK)) < at_lane((NBLK, NBLK))
    later = at_row((NBLK, NBLK)) > at_lane((NBLK, NBLK))
    blks = []
    for part in range(3):
        place, core = split(goal >> 3)
        member = place[ORDER[part][0]] * 2 + core
        place, core = split(goal_col >> 3)
        member_col = place[ORDER[part][0]] * 2 + core
        pos = down(1, (member_col == member) & earlier)
        pos_col = across(1, (member_col == member) & later)
        most = jnp.maximum(most, pos + 1)
        rows.append(member * MOST + pos)
        slot_col = member_col * MOST + pos_col
        for side in range(2):
            hit = slot_col == at_lane((NBLK, W)) + side * W
            blks.append(down(at_row((NBLK, W)), hit))
    order, same, end = sort_tables(source, column(source), TILES, NBLK)
    return rows + blks + [order, same, end], most


SLOT, BLK, BY_SOURCE, SAME, END, OWN_ROWS = 0, 3, 9, 10, 11, 16


def group_tables(part, goals, mine, my_core):
    first, second, third = ORDER[part]
    place, core = split(goals >> 3)
    picked = jnp.where((place[first] == mine[first]) & (core == my_core), 1, 0)
    dense = place[second] * 32 + place[third] * 8 + (goals & 7)
    pos = picked
    step = 1
    while step < NBLK:
        pos = pos + jnp.where(at_lane(pos.shape) >= step, pltpu.roll(pos, step, 1), 0)
        step *= 2
    pos = jnp.where(picked > 0, pos - 1, NBLK)
    k = at_row((MOST, NBLK))
    want = jnp.concatenate(
        [across(dense[m:m + 1] + 1, pos[m:m + 1] == k) for m in range(8)], axis=0) - 1
    key = jnp.where(want < 0, 1000, want)
    key_row = line(key)
    perm, keep, last = sort_tables(key_row, key, DENSE, 8 * MOST)
    want_row = jnp.where(key_row == 1000, 0, key_row)
    rows = []
    for one in (perm, keep, want_row):
        rows += [one[:, :W], one[:, W:]]
    return rows + [last]


PERM, KEEP, WANT, LAST, GROUP_ROWS = 0, 2, 4, 6, 24


def wait_in(ref, sem):
    pltpu.make_async_copy(ref, ref, sem).wait()


def body(cap, halves, unrolled, plan, src, valid, goal, source, ice_in, ocean, mask, rate, weights, ice_out, flux_out, over, *rest):
    rest = list(rest)

    def take(count):
        out = rest[:count]
        del rest[:count]
        return out

    count = len(halves)
    a_send, a_recv, r_send, r_recv, g_send, g_recv, m_send, m_recv, t_sem = rest[-9:]
    del rest[-9:]
    said, heard, own_v, group_v, own_s, group_s, vote_y, vote_z = rest[-8:]
    del rest[-8:]
    refs = [[take(1)[0] for unused in range(3)] + [take(3) for unused in range(12)] for half in range(count)]
    my_ice, my_ocn = lax.axis_index("ice"), lax.axis_index("ocn")
    x, core = my_ice // 2, my_ice % 2
    spot = (x, my_ocn % 4, my_ocn // 4)

    def device(axis, step, which):
        place = list(spot)
        place[axis] = (place[axis] + step + 4) % 4
        return (place[0] * 2 + which, place[2] * 4 + place[1])

    def push(src, dst, send, recv, to):
        copy = pltpu.make_async_remote_copy(src, dst, send, recv, device_id=to, device_id_type=MESH)
        copy.start()
        return copy

    def drain(copies):
        for copy in copies:
            copy.wait_send()
        copies.clear()

    def loop(size, unroll, one):
        def few(k, carry):
            one(k)
            return carry

        lax.fori_loop(0, size, few, 0, unroll=unroll)

    barrier = pltpu.get_barrier_semaphore()
    peers = [(my_ice // 2 * 2 + 1 - core, my_ocn)]
    for axis in range(3):
        for step in (1, -1):
            peers += [device(axis, step, 0), device(axis, step, 1)]
        peers += [device(axis, 2, 0), device(axis, 2, 1)]
    for peer in peers:
        pl.semaphore_signal(barrier, inc=1, device_id=peer, device_id_type=MESH)
    top = 0
    tops = []
    for half, rows in enumerate(halves):
        ice_t, prod, pre = refs[half][:3]
        tall = sum(rows)
        tops.append(top)
        for tile in range(TILES):
            lanes = slice(tile * W, (tile + 1) * W)
            ice_t[tile] = (ice_in[top:top + tall, lanes].astype(F32) * mask[:, lanes]).astype(BF16)
        for part in range(3):
            refs[half][8][part][8 * MOST] = jnp.zeros((rows[part], W), BF16)
        pre[NBLK] = jnp.zeros((tall, W), F32)
        top += tall
    tables, most = own_tables(goal[...], source[...])
    for row, one in enumerate(tables):
        own_v[row:row + 1] = one
    moved = pltpu.make_async_copy(own_v, own_s, t_sem.at[0])
    moved.start()
    said[0] = goal[...] + jnp.where(jnp.max(most, axis=1, keepdims=True) > cap, 1024, 0)
    for part in range(3):
        heard[part, spot[ORDER[part][0]] * 2 + core] = said[0]
    pl.semaphore_wait(barrier, len(peers))
    told = []
    for part in range(3):
        axis = ORDER[part][0]
        me = spot[axis] * 2 + core
        for turn, (step, flip) in enumerate(((0, 1), (1, 0), (1, 1), (2, 0), (2, 1), (3, 0), (3, 1))):
            other = 1 - core if flip else core
            told.append(push(
                said.at[0], heard.at[part, me], m_send.at[part, turn], m_recv.at[part, me], device(axis, step, other)))
    moved.wait()

    def listen():
        for part in range(3):
            me = spot[ORDER[part][0]] * 2 + core
            for other in range(1, 8):
                member = (me + other) % 8
                wait_in(heard.at[part, member], m_recv.at[part, member])
            goals = jnp.concatenate([heard[part, member] for member in range(8)], axis=0)
            if part == 0:
                vote_y[spot[1]] = jnp.max(goals >> 10, axis=0, keepdims=True)
                for step in range(1, 4):
                    told.append(push(
                        vote_y.at[spot[1]], vote_y.at[spot[1]], m_send.at[3, step], m_recv.at[3, spot[1]], device(1, step, core)))
            for row, one in enumerate(group_tables(part, goals & 1023, spot, core)):
                group_v[part * 7 + row:part * 7 + row + 1] = one
        copy = pltpu.make_async_copy(group_v, group_s, t_sem.at[1])
        copy.start()
        for step in range(1, 4):
            other = (spot[1] + step) % 4
            wait_in(vote_y.at[other], m_recv.at[3, other])
        vote_z[spot[2]] = jnp.maximum(jnp.maximum(vote_y[0], vote_y[1]), jnp.maximum(vote_y[2], vote_y[3]))
        for step in range(1, 4):
            told.append(push(
                vote_z.at[spot[2]], vote_z.at[spot[2]], m_send.at[4, step], m_recv.at[4, spot[2]], device(2, step, core)))
        copy.wait()

    def conclude():
        for step in range(1, 4):
            other = (spot[2] + step) % 4
            wait_in(vote_z.at[other], m_recv.at[4, other])
        over[...] = jnp.maximum(jnp.maximum(vote_z[0], vote_z[1]), jnp.maximum(vote_z[2], vote_z[3]))
        drain(told)

    def own_at(row, at):
        return own_s[row + (at >> 7), at & 127]

    def group_at(part, row, at):
        return group_s[part * 7 + row + (at >> 7), at & 127]

    def run(half, final):
        rows, top = halves[half], tops[half]
        tall = sum(rows)
        base = [sum(rows[:part]) for part in range(3)]
        ice_t, prod, pre, out_buf, in_buf, relay, back, back_relay, scan, dense, wide, rs1, rs2, rs3, rs4 = refs[half]
        lane = lax.broadcasted_iota(I32, (tall, W), 1)

        def exchange_start(way, fetch, into, hop):
            copies = []
            for part in range(3):
                q = spot[ORDER[part][0]]

                def fill(k, part=part, q=q):
                    for other in range(8):
                        member = (q * 2 + core + other) % 8
                        ref = out_buf if other else into
                        ref[part][member * MOST + k] = fetch(part, member * MOST + k)

                loop(cap, 1, fill)
                axis = ORDER[part][0]
                for side, step in ((0, 1), (1, -1)):
                    member = (q + 2) % 4 * 2 + side
                    copies.append(push(
                        out_buf[part].at[pl.ds(member * MOST, cap)], hop[part].at[side],
                        a_send.at[half, way, part, side], a_recv.at[half, way, part, 8 + side], device(axis, step, core)))
            for part in range(3):
                axis = ORDER[part][0]
                q = spot[axis]
                me = q * 2 + core
                for turn, (step, which) in enumerate(((1, 0), (-1, 0), (1, 1), (-1, 1), (0, 1 - core))):
                    member = (q + step + 4) % 4 * 2 + which
                    copies.append(push(
                        out_buf[part].at[pl.ds(member * MOST, cap)], into[part].at[pl.ds(me * MOST, cap)],
                        a_send.at[half, way, part, 2 + turn], a_recv.at[half, way, part, me], device(axis, step, which)))
            return copies

        def exchange_next(way, into, hop):
            copies = []
            for part in range(3):
                axis = ORDER[part][0]
                q = spot[axis]
                for side, step in ((0, 1), (1, -1)):
                    wait_in(hop[part].at[side], a_recv.at[half, way, part, 8 + side])
                    origin = (q - step + 4) % 4 * 2 + core
                    copies.append(push(
                        hop[part].at[side], into[part].at[pl.ds(origin * MOST, cap)],
                        a_send.at[half, way, part, 7 + side], a_recv.at[half, way, part, origin], device(axis, step, side)))
            return copies

        def arrive(way, into):
            for part in range(3):
                q = spot[ORDER[part][0]]
                for other in range(1, 8):
                    member = (q * 2 + core + other) % 8
                    wait_in(into[part].at[pl.ds(member * MOST, cap)], a_recv.at[half, way, part, member])

        def scatter_start(part, level, ref, at, n, one, two):
            axis = ORDER[part][1 + level]
            q, mid = spot[axis], n // 2
            send, recv = r_send.at[half, part, level], r_recv.at[half, part, level]
            far, up, down = at + (q + 2) % 4 * n, at + (q + 1) % 4 * n, at + (q + 3) % 4 * n
            there, here = device(axis, 1, core), device(axis, -1, core)
            return [
                push(ref.at[pl.ds(far, mid)], one.at[0], send.at[0], recv.at[0], there),
                push(ref.at[pl.ds(far + mid, mid)], one.at[1], send.at[1], recv.at[1], here),
                push(ref.at[pl.ds(up + mid, mid)], two.at[0, pl.ds(mid, mid)], send.at[2], recv.at[2], there),
                push(ref.at[pl.ds(down, mid)], two.at[1, pl.ds(0, mid)], send.at[3], recv.at[3], here),
            ]

        def scatter_next(part, level, ref, at, n, one, two):
            axis = ORDER[part][1 + level]
            q, mid = spot[axis], n // 2
            send, recv = r_send.at[half, part, level], r_recv.at[half, part, level]
            copies = []
            for side, step, to in ((0, 1, (q + 1) % 4 * n), (1, -1, (q + 3) % 4 * n + mid)):
                wait_in(one.at[side], recv.at[side])

                def join(k, side=side, to=to):
                    ref[at + to + k] = (ref[at + to + k].astype(F32) + one[side, k].astype(F32)).astype(BF16)

                loop(mid, 4, join)
                copies.append(push(
                    ref.at[pl.ds(at + to, mid)], two.at[side, pl.ds(side * mid, mid)],
                    send.at[4 + side], recv.at[4 + side], device(axis, step, core)))
            return copies

        def scatter_end(part, level, n, two):
            mid = n // 2
            recv = r_recv.at[half, part, level]
            wait_in(two.at[0, pl.ds(mid, mid)], recv.at[2])
            wait_in(two.at[1, pl.ds(0, mid)], recv.at[3])
            wait_in(two.at[0, pl.ds(0, mid)], recv.at[4])
            wait_in(two.at[1, pl.ds(mid, mid)], recv.at[5])

        def total(ref, at, two, k):
            return ref[at + k].astype(F32) + two[0, k].astype(F32) + two[1, k].astype(F32)

        def gather_start(part, level, n, at):
            axis = ORDER[part][1 + level]
            q, ref = spot[axis], wide[part]
            send, recv = g_send.at[half, part, level], g_recv.at[half, part, level]
            own = ref.at[pl.ds(at + q * n, n)]
            return [
                push(own, own, send.at[0], recv.at[0], device(axis, 1, core)),
                push(own, own, send.at[1], recv.at[1], device(axis, -1, core)),
            ]

        def gather_next(part, level, n, at):
            axis = ORDER[part][1 + level]
            q, ref, mid = spot[axis], wide[part], n // 2
            send, recv = g_send.at[half, part, level], g_recv.at[half, part, level]
            low, high = at + (q + 3) % 4 * n, at + (q + 1) % 4 * n
            wait_in(ref.at[pl.ds(low, n)], recv.at[0])
            piece = ref.at[pl.ds(low, mid)]
            first = push(piece, piece, send.at[2], recv.at[2], device(axis, 1, core))
            wait_in(ref.at[pl.ds(high, n)], recv.at[1])
            piece = ref.at[pl.ds(high + mid, mid)]
            return [first, push(piece, piece, send.at[3], recv.at[3], device(axis, -1, core))]

        def gather_end(part, level, n, at):
            q, ref, mid = spot[ORDER[part][1 + level]], wide[part], n // 2
            recv = g_recv.at[half, part, level]
            far = at + (q + 2) % 4 * n
            wait_in(ref.at[pl.ds(far, mid)], recv.at[2])
            wait_in(ref.at[pl.ds(far + mid, mid)], recv.at[3])

        def product(b):
            tile = ice_t[src[b]]
            tile = jnp.where(lane < valid[b], tile, jnp.zeros((), BF16))
            prod[b] = jnp.dot(tile, weights[b], preferred_element_type=F32).astype(BF16)

        def product_slot(part, at):
            return prod[own_at(BLK + 2 * part, at), pl.ds(base[part], rows[part])]

        def flux_slot(part, at):
            return wide[part][group_at(part, WANT, at)]

        parts = range(3)
        lines = [spot[ORDER[part][1]] * 32 for part in parts]
        loop(NBLK, 8, product)
        sent = exchange_start(0, product_slot, in_buf, relay)
        yield
        sent += exchange_next(0, in_buf, relay)
        yield
        arrive(0, in_buf)

        def add(group, accs):
            for one in range(4):
                r = group * 4 + one
                new = []
                for part in parts:
                    piece = in_buf[part][group_at(part, PERM, r)].astype(F32)
                    acc = accs[part] * group_at(part, KEEP, r).astype(F32) + piece
                    scan[part][r] = acc.astype(BF16)
                    new.append(acc)
                accs = tuple(new)
            return accs

        lax.fori_loop(0, 2 * cap, add, tuple(jnp.zeros((rows[part], W), F32) for part in parts))
        held = []
        for part in parts:
            def settle(t, part=part):
                dense[part][t] = scan[part][group_at(part, LAST, t)]

            loop(DENSE, 8, settle)
            held += scatter_start(part, 0, dense[part], 0, 32, rs1[part], rs2[part])
        yield
        for part in parts:
            held += scatter_next(part, 0, dense[part], 0, 32, rs1[part], rs2[part])
        yield
        for part in parts:
            scatter_end(part, 0, 32, rs2[part])

            def sum0(k, part=part):
                dense[part][lines[part] + k] = total(dense[part], lines[part], rs2[part], k).astype(BF16)

            loop(32, 4, sum0)
            held += scatter_start(part, 1, dense[part], lines[part], 8, rs3[part], rs4[part])
        yield
        for part in parts:
            held += scatter_next(part, 1, dense[part], lines[part], 8, rs3[part], rs4[part])
        drain(sent)
        yield
        spread_ = []
        for part in parts:
            scatter_end(part, 1, 8, rs4[part])
            at = lines[part] + spot[ORDER[part][2]] * 8
            here = slice(top + base[part], top + base[part] + rows[part])
            for tile in range(TILES):
                lanes = slice(tile * W, (tile + 1) * W)
                come = total(dense[part], at, rs4[part], tile)
                flux = jnp.tanh(come + ocean[here, lanes].astype(F32)).astype(BF16)
                if final:
                    flux_out[here, lanes] = flux
                wide[part][at + tile] = flux
            spread_ += gather_start(part, 1, 8, lines[part])
        yield
        for part in parts:
            spread_ += gather_next(part, 1, 8, lines[part])
        drain(held)
        yield
        for part in parts:
            gather_end(part, 1, 8, lines[part])
            spread_ += gather_start(part, 0, 32, 0)
        yield
        for part in parts:
            spread_ += gather_next(part, 0, 32, 0)
        yield
        for part in parts:
            gather_end(part, 0, 32, 0)
        sent = exchange_start(1, flux_slot, back, back_relay)
        yield
        sent += exchange_next(1, back, back_relay)
        drain(spread_)
        yield
        arrive(1, back)

        def force(group, acc):
            for one in range(4):
                r = group * 4 + one
                b = own_at(BY_SOURCE, r)
                taken = jnp.concatenate([back[part][own_at(SLOT + part, b)] for part in parts], axis=0)
                term = lax.dot_general(taken, weights[b], (((1,), (1,)), ((), ())), preferred_element_type=F32)
                term = jnp.where(lane < valid[b], term, 0.0)
                acc = acc * own_at(SAME, r).astype(F32) + term
                pre[r] = acc
            return acc

        lax.fori_loop(0, NBLK // 4, force, jnp.zeros((tall, W), F32))
        for tile in range(TILES):
            lanes = slice(tile * W, (tile + 1) * W)
            forcing = pre[own_at(END, tile)]
            change = rate[top:top + tall] * jnp.tanh(forcing)
            new = (mask[:, lanes] * (ice_t[tile].astype(F32) + change)).astype(BF16)
            ice_t[tile] = new
            if final:
                ice_out[top:top + tall, lanes] = new
        drain(sent)

    if not unrolled:
        listen()

        def whole(turn, carry):
            for half in range(count):
                for unused in run(half, True):
                    pass
            return carry

        lax.fori_loop(0, 2, whole, 0)
        conclude()
        return

    def both(half):
        yield from run(half, False)
        yield
        yield from run(half, True)

    live = [both(half) for half in range(count)]
    for at, half in enumerate(plan):
        next(live[half], None)
        if at == LISTEN:
            listen()
    for one in live:
        for unused in one:
            pass
    conclude()


def couple(cap, which, halves, unrolled, plan, src, valid, goal, source, ice, ocean, mask, rate, weights):
    cells = TILES * W
    scratch = []
    for rows in halves:
        tall = sum(rows)
        scratch += [pltpu.VMEM((TILES, tall, W), BF16), pltpu.VMEM((NBLK, tall, W), BF16), pltpu.VMEM((NBLK + 1, tall, W), F32)]
        for shape in (
            (8 * MOST,), (8 * MOST,), (2, cap), (8 * MOST,), (2, cap), (8 * MOST + 1,), (DENSE,), (DENSE,),
            (2, 16), (2, 32), (2, 4), (2, 8),
        ):
            scratch += [pltpu.VMEM(shape + (height, W), BF16) for height in rows]
    n = len(halves)
    scratch += [
        pltpu.VMEM((1, 1, NBLK), I32), pltpu.VMEM((3, 8, 1, NBLK), I32),
        pltpu.VMEM((OWN_ROWS, W), I32), pltpu.VMEM((GROUP_ROWS, W), I32),
        pltpu.SMEM((OWN_ROWS, W), I32), pltpu.SMEM((GROUP_ROWS, W), I32),
        pltpu.VMEM((4, 1, NBLK), I32), pltpu.VMEM((4, 1, NBLK), I32),
    ]
    scratch += [
        pltpu.SemaphoreType.DMA((n, 2, 3, 9)), pltpu.SemaphoreType.DMA((n, 2, 3, 10)),
        pltpu.SemaphoreType.DMA((n, 3, 2, 6)), pltpu.SemaphoreType.DMA((n, 3, 2, 6)),
        pltpu.SemaphoreType.DMA((n, 3, 2, 4)), pltpu.SemaphoreType.DMA((n, 3, 2, 4)),
        pltpu.SemaphoreType.DMA((5, 8)), pltpu.SemaphoreType.DMA((5, 8)), pltpu.SemaphoreType.DMA((2,)),
    ]
    vmem = pl.BlockSpec(memory_space=pltpu.VMEM)
    return pl.pallas_call(
        functools.partial(body, cap, halves, unrolled, plan),
        out_shape=(
            jax.ShapeDtypeStruct((CH, cells), BF16), jax.ShapeDtypeStruct((CH, cells), BF16), jax.ShapeDtypeStruct((1, NBLK), I32)
        ),
        in_specs=[pl.BlockSpec(memory_space=pltpu.SMEM)] * 2 + [vmem] * 7,
        out_specs=(vmem, vmem, vmem),
        scratch_shapes=scratch,
        compiler_params=pltpu.CompilerParams(
            collective_id=which, has_side_effects=True, vmem_limit_bytes=66 * 1024 * 1024 - 2200000
        ),
    )(src, valid, goal, source, ice, ocean, mask, rate, weights)


def on_device(ice_state, ocean_state, ice_rate, block_weights, block_route, block_tiles, block_valid, ice_mask):
    cats, fields, cells = ice_state.shape
    chans = cats * fields
    source = block_tiles[:, 0]
    goal = (block_route[:, 0] * TILES + block_tiles[:, 1]).reshape(1, NBLK)
    grow = ((0, CH - chans), (0, 0))
    ice = jnp.pad(ice_state.reshape(chans, cells), grow)
    ocean = jnp.pad(ocean_state.reshape(chans, cells), grow)
    rate = jnp.pad(ice_rate.reshape(chans, 1), grow)
    mask = ice_mask.astype(F32)[None, :]
    given = source, block_valid, goal, source.reshape(1, NBLK), ice, ocean, mask, rate, block_weights
    ice, flux, over = couple(FEW, 0, HALVES, True, PLAN, *given)

    def again(ice, flux, *given):
        ice, flux, unused = couple(MOST, 1, (ROWS,), False, (), *given)
        return ice, flux

    def keep(ice, flux, *given):
        return ice, flux

    ice, flux = lax.cond(jnp.max(over) > 0, again, keep, ice, flux, *given)
    return ice[:chans].reshape(cats, fields, cells), flux[:chans].reshape(cats, fields, cells)


def solution(mesh):
    placed = (
        P(None, None, ("ice", "ocn")),
        P(None, None, ("ice", "ocn")),
        P(),
        P(("ice", "ocn"), None, None),
        P(("ice", "ocn"), None),
        P(("ice", "ocn"), None),
        P(("ice", "ocn")),
        P(("ice", "ocn")),
    )
    return jax.shard_map(
        on_device,
        mesh=mesh,
        in_specs=placed,
        out_specs=(P(None, None, ("ice", "ocn")), P(None, None, ("ice", "ocn"))),
        check_vma=False,
    )
```

time: 530 us -> 212 us (0.40)
  waiting for transfers between devices: 247 us -> 0 us
  Pallas kernels: 0 us -> 200 us
  local copies, waits for them, and re-layouts: 122 us -> 8.09 us
  blocking collectives: 82.4 us -> 0 us
  matrix products: 35.4 us -> 0 us
  starting transfers between devices: 33.6 us -> 0 us
    all_to_all x4 -> x0, waiting for transfers between devices: 247 us -> none  [the longest x2 165 us: back_move(): lax.all_to_all(buffer, ('ice', 'ocn'), split_axis=0, concat_axis=0, tiled...]
    pallas_call x0 -> x1, Pallas kernels: none -> 200 us  [couple(): pl.pallas_call(functools.partial(body, cap, halves, unrolled, plan), out_...]
    all_to_all x1 -> x0, blocking collectives: 82.4 us -> none  [forward_move(): lax.all_to_all(buffer, ('ice', 'ocn'), split_axis=0, concat_axis=0, tiled...]
    scatter x3 -> x0, local copies, waits for them, and re-layouts: 36.3 us -> none  [the longest x2 35.3 us: on_device(): jnp.zeros((devices * CAP, chans, width), jnp.bfloat16).at[place].set(prods)]
    dot_general x9 -> x0, matrix products: 35.4 us -> none  [the longest x2 12.6 us: on_device(): jnp.einsum('cbi,bio->bco', picked, masked, preferred_element_type=jnp.flo...]
    all_to_all x4 -> x0, starting transfers between devices: 33.6 us -> none  [the longest x2 12.2 us: back_move(): lax.all_to_all(buffer, ('ice', 'ocn'), split_axis=0, concat_axis=0, tiled...]
    reshape x5, local copies, waits for them, and re-layouts: 33.6 us -> 6.06 us  [the longest x1 1.66 us: on_device(): flux[:chans].reshape(cats, fields, cells)]
    all_to_all x6 -> x0, local copies, waits for them, and re-layouts: 27.5 us -> none  [the longest x2 13.5 us: back_move(): lax.all_to_all(buffer, ('ice', 'ocn'), split_axis=0, concat_axis=0, tiled...]
  transfers between devices with their start and end apart: 4 -> 0, of which waited for: 3 -> 0; matrix products, arithmetic and copies ran while one was open for 9% -> 0% of each run, Pallas kernels for 0% -> 0%
where the time goes in v3:
time: 212 us
  Pallas kernels  200 us (94%)
  local copies, waits for them, and re-layouts  8.09 us (4%)
  other arithmetic  2.72 us (1%)
    pallas_call x1, Pallas kernels, couple(): pl.pallas_call(functools.partial(body, cap, halves, unrolled, plan), out_...  200 us

profile of v3, /device:TPU:0, one launch (start us, length us, event | category | flops | bytes accessed | tf_op | source)
XLA Modules:
  0.0 212.0 jit_solution(300753882847992591)
XLA Ops:
  0.6 0.0 copy-start
  0.6 0.8 slice_bitcast_fusion
  1.4 0.7 convert_element_type.11
  2.1 0.8 reshape.60
  2.9 0.6 pad.13.rate
  3.5 1.0 reshape.51
  4.5 0.7 pad.11.ice_in
  5.2 1.0 reshape.52
  6.2 0.7 pad.12.ocean
  6.9 199.9 %shard_map.95 = (bf16[104,1024]{1,0:T(8,128)(2,1)}, bf16[104,1024]{1,0:T(8,128)(2,1)}, s32[1,128]{1,0:T(1,128)}) custom-call(s32[128]{0:T(128)S(1)} %get-tuple-element.55.src, s32[128]{0:T(128)} %valid.1, s32[1,128]{1,0:T(1,128)S(1)} %get-tuple-element.54.goal, s32[1,128]{1,0:T(1,128)S(1)} %get-tuple-element.53.source, bf16[104,1024]{1,0:T(8,128)(2,1)} %pad.11.ice_in, ...), custom_call_target="tpu_custom_call" | custom-call | tf_op jit(solution)/shard_map/pallas_call | solution.py:545
  206.8 1.3 reduce_max.9
  208.7 0.0 copy-done
  208.7 3.3 %conditional.1 = (bf16[5,20,1024]{2,1,0:T(8,128)(2,1)}, bf16[5,20,1024]{2,1,0:T(8,128)(2,1)}) conditional(s32[]{:T(128)} %convert_element_type.12, (bf16[104,1024]{1,0:T(8,128)(2,1)}, bf16[104,1024]{1,0:T(8,128)(2,1)}) %tuple.19, (s32[128]{0:T(128)S(1)}, s32[128]{0:T(128)S(1)}, s32[1,128]{1,0:T(1,128)S(1)}, s32[1,128]{1,0:T(1,128)S(1)}, ...), branch_computations={%region_1.2_spmd, %region_2.3_spmd} | conditional | bytes 819216 | solution.py:579
  208.7 1.7 reshape.58
  210.4 1.7 reshape.56
Async XLA Ops:
  0.6 208.1 %copy-start = (s32[128]{0:T(128)S(1)}, s32[128]{0:T(128)}, u32[]{:S(2)}) copy-start(s32[128]{0:T(128)} %valid.1) | copy-start | bytes 1540

commit v4 on v3

--- a/solution.py
+++ b/solution.py
@@ -12,19 +12,20 @@
 BF16 = jnp.bfloat16
 I32 = jnp.int32
 
-ROWS = (32, 32, 40)
-HALVES = ((16, 16, 16), (16, 16, 24))
-LEAD = 1
-PLAN = (0,) * LEAD + (0, 1) * 40
-LISTEN = 1
-CH = 104
+ROWS = (32, 32, 32, 4)
+PARTS = len(ROWS)
+TABLE = (0, 1, 2, 1)
+HALVES = (ROWS,)
+PLAN = tuple(int(one) for one in "0")
+LISTEN = 0
+CH = 100
 NBLK = 128
 TILES = 8
 W = 128
 MOST = 32
 FEW = 20
 DENSE = 128
-ORDER = ((0, 1, 2), (1, 2, 0), (2, 0, 1))
+ORDER = ((0, 1, 2), (1, 2, 0), (2, 0, 1), (1, 2, 0))
 
 
 def split(owner):
@@ -131,7 +132,7 @@
     pltpu.make_async_copy(ref, ref, sem).wait()
 
 
-def body(cap, halves, unrolled, plan, src, valid, goal, source, ice_in, ocean, mask, rate, weights, ice_out, flux_out, over, *rest):
+def body(cap, halves, unrolled, plan, src, valid, goal, source, ice_in, ocean, mask, rate, blocks, ice_out, flux_out, over, *rest):
     rest = list(rest)
 
     def take(count):
@@ -142,9 +143,11 @@
     count = len(halves)
     a_send, a_recv, r_send, r_recv, g_send, g_recv, m_send, m_recv, t_sem = rest[-9:]
     del rest[-9:]
-    said, heard, own_v, group_v, own_s, group_s, vote_y, vote_z = rest[-8:]
-    del rest[-8:]
-    refs = [[take(1)[0] for unused in range(3)] + [take(3) for unused in range(12)] for half in range(count)]
+    said, heard, own_v, group_v, own_s, group_s, vote_y, vote_z, weights, turned = rest[-10:]
+    del rest[-10:]
+    loading = pltpu.make_async_copy(blocks, weights, t_sem.at[2])
+    loading.start()
+    refs = [[take(1)[0] for unused in range(3)] + [take(PARTS) for unused in range(12)] for half in range(count)]
     my_ice, my_ocn = lax.axis_index("ice"), lax.axis_index("ocn")
     x, core = my_ice // 2, my_ice % 2
     spot = (x, my_ocn % 4, my_ocn // 4)
@@ -188,7 +191,7 @@
         for tile in range(TILES):
             lanes = slice(tile * W, (tile + 1) * W)
             ice_t[tile] = (ice_in[top:top + tall, lanes].astype(F32) * mask[:, lanes]).astype(BF16)
-        for part in range(3):
+        for part in range(PARTS):
             refs[half][8][part][8 * MOST] = jnp.zeros((rows[part], W), BF16)
         pre[NBLK] = jnp.zeros((tall, W), F32)
         top += tall
@@ -209,7 +212,9 @@
             other = 1 - core if flip else core
             told.append(push(
                 said.at[0], heard.at[part, me], m_send.at[part, turn], m_recv.at[part, me], device(axis, step, other)))
-    moved.wait()
+    loading.wait()
+    if not unrolled:
+        moved.wait()
 
     def listen():
         for part in range(3):
@@ -236,45 +241,47 @@
                 vote_z.at[spot[2]], vote_z.at[spot[2]], m_send.at[4, step], m_recv.at[4, spot[2]], device(2, step, core)))
         copy.wait()
 
+        def turn_round(b):
+            turned[b] = weights[b].T
+
+        loop(NBLK, 4, turn_round)
+
     def conclude():
         for step in range(1, 4):
             other = (spot[2] + step) % 4
             wait_in(vote_z.at[other], m_recv.at[4, other])
-        over[...] = jnp.maximum(jnp.maximum(vote_z[0], vote_z[1]), jnp.maximum(vote_z[2], vote_z[3]))
+        over[0] = jnp.max(jnp.maximum(jnp.maximum(vote_z[0], vote_z[1]), jnp.maximum(vote_z[2], vote_z[3])))
         drain(told)
-
-    def own_at(row, at):
-        return own_s[row + (at >> 7), at & 127]
-
-    def group_at(part, row, at):
-        return group_s[part * 7 + row + (at >> 7), at & 127]
 
     def run(half, final):
         rows, top = halves[half], tops[half]
         tall = sum(rows)
-        base = [sum(rows[:part]) for part in range(3)]
+        base = [sum(rows[:part]) for part in range(PARTS)]
         ice_t, prod, pre, out_buf, in_buf, relay, back, back_relay, scan, dense, wide, rs1, rs2, rs3, rs4 = refs[half]
         lane = lax.broadcasted_iota(I32, (tall, W), 1)
 
         def exchange_start(way, fetch, into, hop):
             copies = []
-            for part in range(3):
+            for part in range(PARTS):
                 q = spot[ORDER[part][0]]
 
-                def fill(k, part=part, q=q):
+                members = [(q * 2 + core + other) % 8 for other in range(8)]
+                lines_of = [(member // 4, member % 4 * MOST, member * MOST) for member in members]
+
+                def fill(k, part=part, lines_of=lines_of):
+                    got = [fetch(part, row, at + k) for row, at, unused in lines_of]
                     for other in range(8):
-                        member = (q * 2 + core + other) % 8
                         ref = out_buf if other else into
-                        ref[part][member * MOST + k] = fetch(part, member * MOST + k)
-
-                loop(cap, 1, fill)
+                        ref[part][lines_of[other][2] + k] = got[other]
+
+                loop(cap, 2, fill)
                 axis = ORDER[part][0]
                 for side, step in ((0, 1), (1, -1)):
                     member = (q + 2) % 4 * 2 + side
                     copies.append(push(
                         out_buf[part].at[pl.ds(member * MOST, cap)], hop[part].at[side],
                         a_send.at[half, way, part, side], a_recv.at[half, way, part, 8 + side], device(axis, step, core)))
-            for part in range(3):
+            for part in range(PARTS):
                 axis = ORDER[part][0]
                 q = spot[axis]
                 me = q * 2 + core
@@ -287,7 +294,7 @@
 
         def exchange_next(way, into, hop):
             copies = []
-            for part in range(3):
+            for part in range(PARTS):
                 axis = ORDER[part][0]
                 q = spot[axis]
                 for side, step in ((0, 1), (1, -1)):
@@ -298,46 +305,46 @@
                         a_send.at[half, way, part, 7 + side], a_recv.at[half, way, part, origin], device(axis, step, side)))
             return copies
 
-        def arrive(way, into):
-            for part in range(3):
-                q = spot[ORDER[part][0]]
-                for other in range(1, 8):
-                    member = (q * 2 + core + other) % 8
-                    wait_in(into[part].at[pl.ds(member * MOST, cap)], a_recv.at[half, way, part, member])
-
-        def scatter_start(part, level, ref, at, n, one, two):
-            axis = ORDER[part][1 + level]
+        def arrive(way, part, into):
+            q = spot[ORDER[part][0]]
+            for other in range(1, 8):
+                member = (q * 2 + core + other) % 8
+                wait_in(into[part].at[pl.ds(member * MOST, cap)], a_recv.at[half, way, part, member])
+
+        def scatter_far(part, key, axis, ref, at, stride, one, n):
             q, mid = spot[axis], n // 2
-            send, recv = r_send.at[half, part, level], r_recv.at[half, part, level]
-            far, up, down = at + (q + 2) % 4 * n, at + (q + 1) % 4 * n, at + (q + 3) % 4 * n
-            there, here = device(axis, 1, core), device(axis, -1, core)
+            far = at + (q + 2) % 4 * stride
+            send, recv = r_send.at[half, part, key], r_recv.at[half, part, key]
             return [
-                push(ref.at[pl.ds(far, mid)], one.at[0], send.at[0], recv.at[0], there),
-                push(ref.at[pl.ds(far + mid, mid)], one.at[1], send.at[1], recv.at[1], here),
-                push(ref.at[pl.ds(up + mid, mid)], two.at[0, pl.ds(mid, mid)], send.at[2], recv.at[2], there),
-                push(ref.at[pl.ds(down, mid)], two.at[1, pl.ds(0, mid)], send.at[3], recv.at[3], here),
+                push(ref.at[pl.ds(far, mid)], one.at[0], send.at[0], recv.at[0], device(axis, 1, core)),
+                push(ref.at[pl.ds(far + mid, mid)], one.at[1], send.at[1], recv.at[1], device(axis, -1, core)),
             ]
 
-        def scatter_next(part, level, ref, at, n, one, two):
-            axis = ORDER[part][1 + level]
+        def scatter_near(part, key, axis, ref, at, stride, two, n):
             q, mid = spot[axis], n // 2
-            send, recv = r_send.at[half, part, level], r_recv.at[half, part, level]
+            up, below = at + (q + 1) % 4 * stride, at + (q + 3) % 4 * stride
+            send, recv = r_send.at[half, part, key], r_recv.at[half, part, key]
+            return [
+                push(ref.at[pl.ds(up + mid, mid)], two.at[0, pl.ds(mid, mid)], send.at[2], recv.at[2], device(axis, 1, core)),
+                push(ref.at[pl.ds(below, mid)], two.at[1, pl.ds(0, mid)], send.at[3], recv.at[3], device(axis, -1, core)),
+            ]
+
+        def scatter_next(part, key, axis, ref, at, stride, one, two, n):
+            q, mid = spot[axis], n // 2
+            send, recv = r_send.at[half, part, key], r_recv.at[half, part, key]
             copies = []
-            for side, step, to in ((0, 1, (q + 1) % 4 * n), (1, -1, (q + 3) % 4 * n + mid)):
+            for side, step, to in ((0, 1, at + (q + 1) % 4 * stride), (1, -1, at + (q + 3) % 4 * stride + mid)):
                 wait_in(one.at[side], recv.at[side])
-
-                def join(k, side=side, to=to):
-                    ref[at + to + k] = (ref[at + to + k].astype(F32) + one[side, k].astype(F32)).astype(BF16)
-
-                loop(mid, 4, join)
+                for k in range(mid):
+                    ref[to + k] = (ref[to + k].astype(F32) + one[side, k].astype(F32)).astype(BF16)
                 copies.append(push(
-                    ref.at[pl.ds(at + to, mid)], two.at[side, pl.ds(side * mid, mid)],
+                    ref.at[pl.ds(to, mid)], two.at[side, pl.ds(side * mid, mid)],
                     send.at[4 + side], recv.at[4 + side], device(axis, step, core)))
             return copies
 
-        def scatter_end(part, level, n, two):
+        def scatter_end(part, key, two, n):
             mid = n // 2
-            recv = r_recv.at[half, part, level]
+            recv = r_recv.at[half, part, key]
             wait_in(two.at[0, pl.ds(mid, mid)], recv.at[2])
             wait_in(two.at[1, pl.ds(0, mid)], recv.at[3])
             wait_in(two.at[0, pl.ds(0, mid)], recv.at[4])
@@ -346,96 +353,110 @@
         def total(ref, at, two, k):
             return ref[at + k].astype(F32) + two[0, k].astype(F32) + two[1, k].astype(F32)
 
-        def gather_start(part, level, n, at):
-            axis = ORDER[part][1 + level]
+        def gather_start(part, key, axis, at, stride):
             q, ref = spot[axis], wide[part]
-            send, recv = g_send.at[half, part, level], g_recv.at[half, part, level]
-            own = ref.at[pl.ds(at + q * n, n)]
+            send, recv = g_send.at[half, part, key], g_recv.at[half, part, key]
+            own = ref.at[pl.ds(at + q * stride, 8)]
             return [
                 push(own, own, send.at[0], recv.at[0], device(axis, 1, core)),
                 push(own, own, send.at[1], recv.at[1], device(axis, -1, core)),
             ]
 
-        def gather_next(part, level, n, at):
-            axis = ORDER[part][1 + level]
-            q, ref, mid = spot[axis], wide[part], n // 2
-            send, recv = g_send.at[half, part, level], g_recv.at[half, part, level]
-            low, high = at + (q + 3) % 4 * n, at + (q + 1) % 4 * n
-            wait_in(ref.at[pl.ds(low, n)], recv.at[0])
-            piece = ref.at[pl.ds(low, mid)]
+        def gather_next(part, key, axis, at, stride):
+            q, ref = spot[axis], wide[part]
+            send, recv = g_send.at[half, part, key], g_recv.at[half, part, key]
+            low, high = at + (q + 3) % 4 * stride, at + (q + 1) % 4 * stride
+            wait_in(ref.at[pl.ds(low, 8)], recv.at[0])
+            piece = ref.at[pl.ds(low, 4)]
             first = push(piece, piece, send.at[2], recv.at[2], device(axis, 1, core))
-            wait_in(ref.at[pl.ds(high, n)], recv.at[1])
-            piece = ref.at[pl.ds(high + mid, mid)]
+            wait_in(ref.at[pl.ds(high, 8)], recv.at[1])
+            piece = ref.at[pl.ds(high + 4, 4)]
             return [first, push(piece, piece, send.at[3], recv.at[3], device(axis, -1, core))]
 
-        def gather_end(part, level, n, at):
-            q, ref, mid = spot[ORDER[part][1 + level]], wide[part], n // 2
-            recv = g_recv.at[half, part, level]
-            far = at + (q + 2) % 4 * n
-            wait_in(ref.at[pl.ds(far, mid)], recv.at[2])
-            wait_in(ref.at[pl.ds(far + mid, mid)], recv.at[3])
+        def gather_end(part, key, axis, at, stride):
+            q, ref = spot[axis], wide[part]
+            recv = g_recv.at[half, part, key]
+            far = at + (q + 2) % 4 * stride
+            wait_in(ref.at[pl.ds(far, 4)], recv.at[2])
+            wait_in(ref.at[pl.ds(far + 4, 4)], recv.at[3])
 
         def product(b):
             tile = ice_t[src[b]]
             tile = jnp.where(lane < valid[b], tile, jnp.zeros((), BF16))
             prod[b] = jnp.dot(tile, weights[b], preferred_element_type=F32).astype(BF16)
 
-        def product_slot(part, at):
-            return prod[own_at(BLK + 2 * part, at), pl.ds(base[part], rows[part])]
-
-        def flux_slot(part, at):
-            return wide[part][group_at(part, WANT, at)]
-
-        parts = range(3)
-        lines = [spot[ORDER[part][1]] * 32 for part in parts]
+        def product_slot(part, row, at):
+            return prod[own_s[BLK + 2 * TABLE[part] + row, at], pl.ds(base[part], rows[part])]
+
+        def flux_slot(part, row, at):
+            return wide[part][group_s[7 * TABLE[part] + WANT + row, at]]
+
+        parts = range(PARTS)
+        second, third = [ORDER[part][1] for part in parts], [ORDER[part][2] for part in parts]
+        lines = [spot[second[part]] * 32 for part in parts]
         loop(NBLK, 8, product)
+        if unrolled and not final and half == 0:
+            moved.wait()
         sent = exchange_start(0, product_slot, in_buf, relay)
         yield
         sent += exchange_next(0, in_buf, relay)
         yield
-        arrive(0, in_buf)
-
-        def add(group, accs):
-            for one in range(4):
-                r = group * 4 + one
-                new = []
-                for part in parts:
-                    piece = in_buf[part][group_at(part, PERM, r)].astype(F32)
-                    acc = accs[part] * group_at(part, KEEP, r).astype(F32) + piece
-                    scan[part][r] = acc.astype(BF16)
-                    new.append(acc)
-                accs = tuple(new)
-            return accs
-
-        lax.fori_loop(0, 2 * cap, add, tuple(jnp.zeros((rows[part], W), F32) for part in parts))
         held = []
         for part in parts:
-            def settle(t, part=part):
-                dense[part][t] = scan[part][group_at(part, LAST, t)]
-
-            loop(DENSE, 8, settle)
-            held += scatter_start(part, 0, dense[part], 0, 32, rs1[part], rs2[part])
-        yield
-        for part in parts:
-            held += scatter_next(part, 0, dense[part], 0, 32, rs1[part], rs2[part])
-        yield
-        for part in parts:
-            scatter_end(part, 0, 32, rs2[part])
-
-            def sum0(k, part=part):
-                dense[part][lines[part] + k] = total(dense[part], lines[part], rs2[part], k).astype(BF16)
-
-            loop(32, 4, sum0)
-            held += scatter_start(part, 1, dense[part], lines[part], 8, rs3[part], rs4[part])
-        yield
-        for part in parts:
-            held += scatter_next(part, 1, dense[part], lines[part], 8, rs3[part], rs4[part])
+            arrive(0, part, in_buf)
+            acc = jnp.zeros((rows[part], W), F32)
+            for line_, steps in ((0, min(W, 8 * cap)), (1, 8 * cap - W)):
+                def add(group, acc, part=part, line_=line_):
+                    for one in range(8):
+                        r = group * 8 + one
+                        piece = in_buf[part][group_s[7 * TABLE[part] + PERM + line_, r]].astype(F32)
+                        acc = acc * group_s[7 * TABLE[part] + KEEP + line_, r].astype(F32) + piece
+                        scan[part][line_ * W + r] = acc.astype(BF16)
+                    return acc
+
+                acc = lax.fori_loop(0, steps // 8, add, acc)
+            for d in (2, 1, 3, 0):
+                at = (spot[third[part]] + d) % 4 * 8
+
+                def settle(k, part=part, at=at):
+                    got = [scan[part][group_s[7 * TABLE[part] + LAST, k * 32 + at + tile]] for tile in range(8)]
+                    for tile in range(8):
+                        dense[part][k * 32 + at + tile] = got[tile]
+
+                loop(4, 1, settle)
+                held += scatter_far(part, 1 + d, second[part], dense[part], at, 32, rs1[part].at[d], 8)
+                held += scatter_near(part, 1 + d, second[part], dense[part], at, 32, rs2[part].at[d], 8)
+        yield
+        for d in (2, 1, 3, 0):
+            for part in parts:
+                at = (spot[third[part]] + d) % 4 * 8
+                held += scatter_next(part, 1 + d, second[part], dense[part], at, 32, rs1[part].at[d], rs2[part].at[d], 8)
+        yield
+
+        def collect(part, d):
+            scatter_end(part, 1 + d, rs2[part].at[d], 8)
+            at = lines[part] + (spot[third[part]] + d) % 4 * 8
+            for k in range(8):
+                dense[part][at + k] = total(dense[part], at, rs2[part].at[d], k).astype(BF16)
+
+        for part in parts:
+            collect(part, 2)
+            held += scatter_far(part, 0, third[part], dense[part], lines[part], 8, rs3[part], 8)
+        for part in parts:
+            collect(part, 1)
+            collect(part, 3)
+            held += scatter_near(part, 0, third[part], dense[part], lines[part], 8, rs4[part], 8)
+        yield
+        for part in parts:
+            held += scatter_next(part, 0, third[part], dense[part], lines[part], 8, rs3[part], rs4[part], 8)
+        for part in parts:
+            collect(part, 0)
         drain(sent)
         yield
         spread_ = []
         for part in parts:
-            scatter_end(part, 1, 8, rs4[part])
-            at = lines[part] + spot[ORDER[part][2]] * 8
+            scatter_end(part, 0, rs4[part], 8)
+            at = lines[part] + spot[third[part]] * 8
             here = slice(top + base[part], top + base[part] + rows[part])
             for tile in range(TILES):
                 lanes = slice(tile * W, (tile + 1) * W)
@@ -444,43 +465,54 @@
                 if final:
                     flux_out[here, lanes] = flux
                 wide[part][at + tile] = flux
-            spread_ += gather_start(part, 1, 8, lines[part])
-        yield
-        for part in parts:
-            spread_ += gather_next(part, 1, 8, lines[part])
+            spread_ += gather_start(part, 0, third[part], lines[part], 8)
+            spread_ += gather_start(part, 1, second[part], spot[third[part]] * 8, 32)
         drain(held)
         yield
         for part in parts:
-            gather_end(part, 1, 8, lines[part])
-            spread_ += gather_start(part, 0, 32, 0)
-        yield
-        for part in parts:
-            spread_ += gather_next(part, 0, 32, 0)
-        yield
-        for part in parts:
-            gather_end(part, 0, 32, 0)
+            at = [(spot[third[part]] + d) % 4 * 8 for d in range(4)]
+            spread_ += gather_next(part, 0, third[part], lines[part], 8)
+            spread_ += gather_start(part, 2, second[part], at[1], 32)
+            spread_ += gather_start(part, 4, second[part], at[3], 32)
+            spread_ += gather_next(part, 1, second[part], at[0], 32)
+        yield
+        for part in parts:
+            at = [(spot[third[part]] + d) % 4 * 8 for d in range(4)]
+            gather_end(part, 0, third[part], lines[part], 8)
+            spread_ += gather_start(part, 3, second[part], at[2], 32)
+            spread_ += gather_next(part, 2, second[part], at[1], 32)
+            spread_ += gather_next(part, 4, second[part], at[3], 32)
+        yield
+        for part in parts:
+            at = [(spot[third[part]] + d) % 4 * 8 for d in range(4)]
+            spread_ += gather_next(part, 3, second[part], at[2], 32)
+        for part in parts:
+            at = [(spot[third[part]] + d) % 4 * 8 for d in range(4)]
+            for d in range(4):
+                gather_end(part, 1 + d, second[part], at[d], 32)
         sent = exchange_start(1, flux_slot, back, back_relay)
         yield
         sent += exchange_next(1, back, back_relay)
         drain(spread_)
         yield
-        arrive(1, back)
+        for part in parts:
+            arrive(1, part, back)
 
         def force(group, acc):
             for one in range(4):
                 r = group * 4 + one
-                b = own_at(BY_SOURCE, r)
-                taken = jnp.concatenate([back[part][own_at(SLOT + part, b)] for part in parts], axis=0)
-                term = lax.dot_general(taken, weights[b], (((1,), (1,)), ((), ())), preferred_element_type=F32)
+                b = own_s[BY_SOURCE, r]
+                taken = jnp.concatenate([back[part][own_s[SLOT + TABLE[part], b]] for part in parts], axis=0)
+                term = jnp.dot(taken, turned[b], preferred_element_type=F32)
                 term = jnp.where(lane < valid[b], term, 0.0)
-                acc = acc * own_at(SAME, r).astype(F32) + term
+                acc = acc * own_s[SAME, r].astype(F32) + term
                 pre[r] = acc
             return acc
 
         lax.fori_loop(0, NBLK // 4, force, jnp.zeros((tall, W), F32))
         for tile in range(TILES):
             lanes = slice(tile * W, (tile + 1) * W)
-            forcing = pre[own_at(END, tile)]
+            forcing = pre[own_s[END, tile]]
             change = rate[top:top + tall] * jnp.tanh(forcing)
             new = (mask[:, lanes] * (ice_t[tile].astype(F32) + change)).astype(BF16)
             ice_t[tile] = new
@@ -503,7 +535,6 @@
 
     def both(half):
         yield from run(half, False)
-        yield
         yield from run(half, True)
 
     live = [both(half) for half in range(count)]
@@ -525,7 +556,7 @@
         scratch += [pltpu.VMEM((TILES, tall, W), BF16), pltpu.VMEM((NBLK, tall, W), BF16), pltpu.VMEM((NBLK + 1, tall, W), F32)]
         for shape in (
             (8 * MOST,), (8 * MOST,), (2, cap), (8 * MOST,), (2, cap), (8 * MOST + 1,), (DENSE,), (DENSE,),
-            (2, 16), (2, 32), (2, 4), (2, 8),
+            (4, 2, 4), (4, 2, 8), (2, 4), (2, 8),
         ):
             scratch += [pltpu.VMEM(shape + (height, W), BF16) for height in rows]
     n = len(halves)
@@ -534,21 +565,22 @@
         pltpu.VMEM((OWN_ROWS, W), I32), pltpu.VMEM((GROUP_ROWS, W), I32),
         pltpu.SMEM((OWN_ROWS, W), I32), pltpu.SMEM((GROUP_ROWS, W), I32),
         pltpu.VMEM((4, 1, NBLK), I32), pltpu.VMEM((4, 1, NBLK), I32),
+        pltpu.VMEM((NBLK, W, W), BF16), pltpu.VMEM((NBLK, W, W), BF16),
     ]
     scratch += [
-        pltpu.SemaphoreType.DMA((n, 2, 3, 9)), pltpu.SemaphoreType.DMA((n, 2, 3, 10)),
-        pltpu.SemaphoreType.DMA((n, 3, 2, 6)), pltpu.SemaphoreType.DMA((n, 3, 2, 6)),
-        pltpu.SemaphoreType.DMA((n, 3, 2, 4)), pltpu.SemaphoreType.DMA((n, 3, 2, 4)),
-        pltpu.SemaphoreType.DMA((5, 8)), pltpu.SemaphoreType.DMA((5, 8)), pltpu.SemaphoreType.DMA((2,)),
+        pltpu.SemaphoreType.DMA((n, 2, PARTS, 9)), pltpu.SemaphoreType.DMA((n, 2, PARTS, 10)),
+        pltpu.SemaphoreType.DMA((n, PARTS, 5, 6)), pltpu.SemaphoreType.DMA((n, PARTS, 5, 6)),
+        pltpu.SemaphoreType.DMA((n, PARTS, 5, 4)), pltpu.SemaphoreType.DMA((n, PARTS, 5, 4)),
+        pltpu.SemaphoreType.DMA((5, 8)), pltpu.SemaphoreType.DMA((5, 8)), pltpu.SemaphoreType.DMA((3,)),
     ]
     vmem = pl.BlockSpec(memory_space=pltpu.VMEM)
     return pl.pallas_call(
         functools.partial(body, cap, halves, unrolled, plan),
         out_shape=(
-            jax.ShapeDtypeStruct((CH, cells), BF16), jax.ShapeDtypeStruct((CH, cells), BF16), jax.ShapeDtypeStruct((1, NBLK), I32)
+            jax.ShapeDtypeStruct((CH, cells), BF16), jax.ShapeDtypeStruct((CH, cells), BF16), jax.ShapeDtypeStruct((1,), I32)
         ),
-        in_specs=[pl.BlockSpec(memory_space=pltpu.SMEM)] * 2 + [vmem] * 7,
-        out_specs=(vmem, vmem, vmem),
+        in_specs=[pl.BlockSpec(memory_space=pltpu.SMEM)] * 2 + [vmem] * 6 + [pl.BlockSpec(memory_space=pl.ANY)],
+        out_specs=(vmem, vmem, pl.BlockSpec(memory_space=pltpu.SMEM)),
         scratch_shapes=scratch,
         compiler_params=pltpu.CompilerParams(
             collective_id=which, has_side_effects=True, vmem_limit_bytes=66 * 1024 * 1024 - 2200000
@@ -561,10 +593,9 @@
     chans = cats * fields
     source = block_tiles[:, 0]
     goal = (block_route[:, 0] * TILES + block_tiles[:, 1]).reshape(1, NBLK)
-    grow = ((0, CH - chans), (0, 0))
-    ice = jnp.pad(ice_state.reshape(chans, cells), grow)
-    ocean = jnp.pad(ocean_state.reshape(chans, cells), grow)
-    rate = jnp.pad(ice_rate.reshape(chans, 1), grow)
+    ice = ice_state.reshape(chans, cells)
+    ocean = ocean_state.reshape(chans, cells)
+    rate = ice_rate.reshape(chans, 1)
     mask = ice_mask.astype(F32)[None, :]
     given = source, block_valid, goal, source.reshape(1, NBLK), ice, ocean, mask, rate, block_weights
     ice, flux, over = couple(FEW, 0, HALVES, True, PLAN, *given)
@@ -576,8 +607,8 @@
     def keep(ice, flux, *given):
         return ice, flux
 
-    ice, flux = lax.cond(jnp.max(over) > 0, again, keep, ice, flux, *given)
-    return ice[:chans].reshape(cats, fields, cells), flux[:chans].reshape(cats, fields, cells)
+    ice, flux = lax.cond(over[0] > 0, again, keep, ice, flux, *given)
+    return ice.reshape(cats, fields, cells), flux.reshape(cats, fields, cells)
 
 
 def solution(mesh):

time: 212 us -> 195 us (0.920)
  Pallas kernels: 200 us -> 184 us
    pallas_call x1, Pallas kernels: 200 us -> 184 us  [couple(): pl.pallas_call(functools.partial(body, cap, halves, unrolled, plan), out_...]
    reshape x5 -> x6, local copies, waits for them, and re-layouts: 6.06 us -> 8.15 us  [the longest x2 3.33 us: on_device(): return (ice.reshape(cats, fields, cells), flux.reshape(cats, fields, cells))]
where the time goes in v4:
time: 195 us
  Pallas kernels  184 us (94%)
  local copies, waits for them, and re-layouts  8.16 us (4%)
    pallas_call x1, Pallas kernels, couple(): pl.pallas_call(functools.partial(body, cap, halves, unrolled, plan), out_...  184 us

profile of v4, /device:TPU:0, one launch (start us, length us, event | category | flops | bytes accessed | tf_op | source)
XLA Modules:
  0.0 195.1 jit_solution(13652301298575628425)
XLA Ops:
  0.6 0.0 copy-start
  0.6 0.8 reshape.57
  1.4 0.8 slice_bitcast_fusion
  2.2 0.7 convert_element_type.9
  2.9 0.7 copy.10.rate
  3.6 1.7 reshape.55.ice_in
  5.2 1.7 reshape.56.ocean
  6.9 184.0 %shard_map.95 = (bf16[100,1024]{1,0:T(8,128)(2,1)}, bf16[100,1024]{1,0:T(8,128)(2,1)}, s32[1]{0:T(128)}) custom-call(s32[128]{0:T(128)S(1)} %get-tuple-element.64.src, s32[128]{0:T(128)} %valid.1, s32[1,128]{1,0:T(1,128)S(1)} %get-tuple-element.63.goal, s32[1,128]{1,0:T(1,128)S(1)} %get-tuple-element.62.source, bf16[100,1024]{1,0:T(8,128)(2,1)} %reshape.55.ice_in, ...), custom_call_target="tpu_custom_call" | custom-call | tf_op jit(solution)/shard_map/pallas_call | solution.py:577
  191.5 0.0 copy-done
  191.5 3.5 %conditional.1 = (bf16[5,20,1024]{2,1,0:T(8,128)(2,1)}, bf16[5,20,1024]{2,1,0:T(8,128)(2,1)}) conditional(s32[]{:T(128)} %bitcast.4, (bf16[100,1024]{1,0:T(8,128)(2,1)}, bf16[100,1024]{1,0:T(8,128)(2,1)}) %tuple.19, (s32[128]{0:T(128)S(1)}, s32[128]{0:T(128)S(1)}, s32[1,128]{1,0:T(1,128)S(1)}, s32[1,128]{1,0:T(1,128)S(1)}, ...), branch_computations={%region_0.0_spmd, %region_1.0_spmd} | conditional | bytes 820016 | solution.py:610
  191.7 1.7 reshape.61
  193.4 1.7 reshape.63
Async XLA Ops:
  0.6 190.9 %copy-start = (s32[128]{0:T(128)S(1)}, s32[128]{0:T(128)}, u32[]{:S(2)}) copy-start(s32[128]{0:T(128)} %valid.1) | copy-start | bytes 1540

commit v5 on v4

--- a/solution.py
+++ b/solution.py
@@ -143,8 +143,8 @@
     count = len(halves)
     a_send, a_recv, r_send, r_recv, g_send, g_recv, m_send, m_recv, t_sem = rest[-9:]
     del rest[-9:]
-    said, heard, own_v, group_v, own_s, group_s, vote_y, vote_z, weights, turned = rest[-10:]
-    del rest[-10:]
+    said, heard, own_v, group_v, own_s, group_s, vote_y, vote_z, weights, turned, sea = rest[-11:]
+    del rest[-11:]
     loading = pltpu.make_async_copy(blocks, weights, t_sem.at[2])
     loading.start()
     refs = [[take(1)[0] for unused in range(3)] + [take(PARTS) for unused in range(12)] for half in range(count)]
@@ -182,6 +182,18 @@
         peers += [device(axis, 2, 0), device(axis, 2, 1)]
     for peer in peers:
         pl.semaphore_signal(barrier, inc=1, device_id=peer, device_id_type=MESH)
+    cats, fields, unused = ice_in.shape
+
+    def stacked(ref, lanes):
+        return jnp.concatenate([ref[cat, :, lanes].astype(F32) for cat in range(cats)], axis=0)
+
+    def unstack(ref, lanes, full):
+        for cat in range(cats):
+            ref[cat, :, lanes] = full[cat * fields:(cat + 1) * fields].astype(BF16)
+
+    for tile in range(TILES):
+        lanes = slice(tile * W, (tile + 1) * W)
+        sea[tile] = stacked(ocean, lanes).astype(BF16)
     top = 0
     tops = []
     for half, rows in enumerate(halves):
@@ -190,7 +202,7 @@
         tops.append(top)
         for tile in range(TILES):
             lanes = slice(tile * W, (tile + 1) * W)
-            ice_t[tile] = (ice_in[top:top + tall, lanes].astype(F32) * mask[:, lanes]).astype(BF16)
+            ice_t[tile] = (stacked(ice_in, lanes)[top:top + tall] * mask[:, lanes]).astype(BF16)
         for part in range(PARTS):
             refs[half][8][part][8 * MOST] = jnp.zeros((rows[part], W), BF16)
         pre[NBLK] = jnp.zeros((tall, W), F32)
@@ -459,12 +471,8 @@
             at = lines[part] + spot[third[part]] * 8
             here = slice(top + base[part], top + base[part] + rows[part])
             for tile in range(TILES):
-                lanes = slice(tile * W, (tile + 1) * W)
                 come = total(dense[part], at, rs4[part], tile)
-                flux = jnp.tanh(come + ocean[here, lanes].astype(F32)).astype(BF16)
-                if final:
-                    flux_out[here, lanes] = flux
-                wide[part][at + tile] = flux
+                wide[part][at + tile] = jnp.tanh(come + sea[tile, here].astype(F32)).astype(BF16)
             spread_ += gather_start(part, 0, third[part], lines[part], 8)
             spread_ += gather_start(part, 1, second[part], spot[third[part]] * 8, 32)
         drain(held)
@@ -517,7 +525,9 @@
             new = (mask[:, lanes] * (ice_t[tile].astype(F32) + change)).astype(BF16)
             ice_t[tile] = new
             if final:
-                ice_out[top:top + tall, lanes] = new
+                unstack(ice_out, lanes, new.astype(F32))
+                full = [wide[part][lines[part] + spot[third[part]] * 8 + tile].astype(F32) for part in parts]
+                unstack(flux_out, lanes, jnp.concatenate(full, axis=0))
         drain(sent)
 
     if not unrolled:
@@ -549,7 +559,7 @@
 
 
 def couple(cap, which, halves, unrolled, plan, src, valid, goal, source, ice, ocean, mask, rate, weights):
-    cells = TILES * W
+    result = jax.ShapeDtypeStruct(ice.shape, BF16)
     scratch = []
     for rows in halves:
         tall = sum(rows)
@@ -565,7 +575,7 @@
         pltpu.VMEM((OWN_ROWS, W), I32), pltpu.VMEM((GROUP_ROWS, W), I32),
         pltpu.SMEM((OWN_ROWS, W), I32), pltpu.SMEM((GROUP_ROWS, W), I32),
         pltpu.VMEM((4, 1, NBLK), I32), pltpu.VMEM((4, 1, NBLK), I32),
-        pltpu.VMEM((NBLK, W, W), BF16), pltpu.VMEM((NBLK, W, W), BF16),
+        pltpu.VMEM((NBLK, W, W), BF16), pltpu.VMEM((NBLK, W, W), BF16), pltpu.VMEM((TILES, CH, W), BF16),
     ]
     scratch += [
         pltpu.SemaphoreType.DMA((n, 2, PARTS, 9)), pltpu.SemaphoreType.DMA((n, 2, PARTS, 10)),
@@ -577,7 +587,7 @@
     return pl.pallas_call(
         functools.partial(body, cap, halves, unrolled, plan),
         out_shape=(
-            jax.ShapeDtypeStruct((CH, cells), BF16), jax.ShapeDtypeStruct((CH, cells), BF16), jax.ShapeDtypeStruct((1,), I32)
+            result, result, jax.ShapeDtypeStruct((1,), I32)
         ),
         in_specs=[pl.BlockSpec(memory_space=pltpu.SMEM)] * 2 + [vmem] * 6 + [pl.BlockSpec(memory_space=pl.ANY)],
         out_specs=(vmem, vmem, pl.BlockSpec(memory_space=pltpu.SMEM)),
@@ -593,11 +603,9 @@
     chans = cats * fields
     source = block_tiles[:, 0]
     goal = (block_route[:, 0] * TILES + block_tiles[:, 1]).reshape(1, NBLK)
-    ice = ice_state.reshape(chans, cells)
-    ocean = ocean_state.reshape(chans, cells)
     rate = ice_rate.reshape(chans, 1)
     mask = ice_mask.astype(F32)[None, :]
-    given = source, block_valid, goal, source.reshape(1, NBLK), ice, ocean, mask, rate, block_weights
+    given = source, block_valid, goal, source.reshape(1, NBLK), ice_state, ocean_state, mask, rate, block_weights
     ice, flux, over = couple(FEW, 0, HALVES, True, PLAN, *given)
 
     def again(ice, flux, *given):
@@ -608,7 +616,7 @@
         return ice, flux
 
     ice, flux = lax.cond(over[0] > 0, again, keep, ice, flux, *given)
-    return ice.reshape(cats, fields, cells), flux.reshape(cats, fields, cells)
+    return ice, flux
 
 
 def solution(mesh):

time: 195 us -> 191 us (0.979)
  local copies, waits for them, and re-layouts: 8.16 us -> 4.81 us
    reshape x4 -> x0, local copies, waits for them, and re-layouts: 6.65 us -> none  [the longest x2 3.33 us: on_device(): return (ice.reshape(cats, fields, cells), flux.reshape(cats, fields, cells))]
    unnamed x2 -> x4, local copies, waits for them, and re-layouts: 0.01 us -> 3.31 us
where the time goes in v5:
time: 191 us
  Pallas kernels  183 us (96%)
  local copies, waits for them, and re-layouts  4.81 us (3%)
    pallas_call x1, Pallas kernels, couple(): pl.pallas_call(functools.partial(body, cap, halves, unrolled, plan), out_...  183 us

profile of v5, /device:TPU:0, one launch (start us, length us, event | category | flops | bytes accessed | tf_op | source)
XLA Modules:
  0.0 190.8 jit_solution(7127489711720281538)
XLA Ops:
  0.6 0.0 copy-start
  0.6 0.8 reshape.35
  1.4 0.8 slice_bitcast_fusion
  2.2 0.7 convert_element_type.9
  2.9 0.7 copy.14.rate
  3.6 183.2 %shard_map.99 = (bf16[5,20,1024]{2,1,0:T(8,128)(2,1)}, bf16[5,20,1024]{2,1,0:T(8,128)(2,1)}, s32[1]{0:T(128)}) custom-call(s32[128]{0:T(128)S(1)} %get-tuple-element.56.src, s32[128]{0:T(128)} %valid.1, s32[1,128]{1,0:T(1,128)S(1)} %get-tuple-element.55.goal, s32[1,128]{1,0:T(1,128)S(1)} %get-tuple-element.54.source, bf16[5,20,1024]{2,1,0:T(8,128)(2,1)} %ice_in.1, ...), custom_call_target="tpu_custom_call" | custom-call | tf_op jit(solution)/shard_map/pallas_call | solution.py:587
  187.4 0.0 copy-done
  187.5 1.7 copy.22
  189.1 1.7 copy.23
  (1 shorter events, 0.0 us)
Async XLA Ops:
  0.6 186.8 %copy-start = (s32[128]{0:T(128)S(1)}, s32[128]{0:T(128)}, u32[]{:S(2)}) copy-start(s32[128]{0:T(128)} %valid.1) | copy-start | bytes 1540

commit v6 on v5

--- a/solution.py
+++ b/solution.py
@@ -272,11 +272,12 @@
         ice_t, prod, pre, out_buf, in_buf, relay, back, back_relay, scan, dense, wide, rs1, rs2, rs3, rs4 = refs[half]
         lane = lax.broadcasted_iota(I32, (tall, W), 1)
 
-        def exchange_start(way, fetch, into, hop):
+        def exchange_start(way, fetch, into, hop, ready=None):
             copies = []
             for part in range(PARTS):
                 q = spot[ORDER[part][0]]
-
+                if ready:
+                    ready(part)
                 members = [(q * 2 + core + other) % 8 for other in range(8)]
                 lines_of = [(member // 4, member % 4 * MOST, member * MOST) for member in members]
 
@@ -494,11 +495,12 @@
         for part in parts:
             at = [(spot[third[part]] + d) % 4 * 8 for d in range(4)]
             spread_ += gather_next(part, 3, second[part], at[2], 32)
-        for part in parts:
-            at = [(spot[third[part]] + d) % 4 * 8 for d in range(4)]
+
+        def gathered(part):
             for d in range(4):
-                gather_end(part, 1 + d, second[part], at[d], 32)
-        sent = exchange_start(1, flux_slot, back, back_relay)
+                gather_end(part, 1 + d, second[part], (spot[third[part]] + d) % 4 * 8, 32)
+
+        sent = exchange_start(1, flux_slot, back, back_relay, gathered)
         yield
         sent += exchange_next(1, back, back_relay)
         drain(spread_)

time: 191 us -> 188 us (0.984)
  Pallas kernels: 183 us -> 180 us
    pallas_call x1, Pallas kernels: 183 us -> 180 us  [couple(): pl.pallas_call(functools.partial(body, cap, halves, unrolled, plan), out_...]
where the time goes in v6:
time: 188 us; the launch traced here: 187 us
  Pallas kernels  180 us (96%)
  local copies, waits for them, and re-layouts  4.81 us (3%)
    pallas_call x1, Pallas kernels, couple(): pl.pallas_call(functools.partial(body, cap, halves, unrolled, plan), out_...  180 us

profile of v6, /device:TPU:0, one launch (start us, length us, event | category | flops | bytes accessed | tf_op | source)
XLA Modules:
  0.0 187.5 jit_solution(9915933795602377104)
XLA Ops:
  0.6 0.0 copy-start
  0.6 0.8 reshape.35
  1.4 0.8 slice_bitcast_fusion
  2.2 0.7 convert_element_type.9
  2.9 0.7 copy.14.rate
  3.6 179.9 %shard_map.99 = (bf16[5,20,1024]{2,1,0:T(8,128)(2,1)}, bf16[5,20,1024]{2,1,0:T(8,128)(2,1)}, s32[1]{0:T(128)}) custom-call(s32[128]{0:T(128)S(1)} %get-tuple-element.56.src, s32[128]{0:T(128)} %valid.1, s32[1,128]{1,0:T(1,128)S(1)} %get-tuple-element.55.goal, s32[1,128]{1,0:T(1,128)S(1)} %get-tuple-element.54.source, bf16[5,20,1024]{2,1,0:T(8,128)(2,1)} %ice_in.1, ...), custom_call_target="tpu_custom_call" | custom-call | tf_op jit(solution)/shard_map/pallas_call | solution.py:589
  184.2 0.0 copy-done
  184.2 1.7 copy.22
  185.8 1.7 copy.23
  (1 shorter events, 0.0 us)
Async XLA Ops:
  0.6 183.5 %copy-start = (s32[128]{0:T(128)S(1)}, s32[128]{0:T(128)}, u32[]{:S(2)}) copy-start(s32[128]{0:T(128)} %valid.1) | copy-start | bytes 1540
